TPU v7x, 768 devices: a whole 4x8x12 slice. The times are simulated.
768 devices in a mesh: wave: 12 (over z), lev: 8 (over y), grp: 8 (over x, core).
Axes of the slice: x: 4, y: 8, z: 12, core: 2. Of those that a mesh axis runs over, the one named last changes fastest.
Arguments:
- spectra: bfloat16 [2, 4, 8, 96, 1024], P(None, None, 'lev', ('wave', 'grp')), may hold values from -6 to 6
- legendre: bfloat16 [96, 1024, 384], P(('wave', 'grp')), may hold values from -0.1875 to 0.1875
- wavenumbers: int32 [96], replicated, may hold values from 0 to 1023, as said below
- quad_weights: float32 [384], replicated, may hold values from 0.5 to 2
- tracers: float32 [8, 8, 384, 4096], P(None, 'lev', ('wave', 'grp')), may hold values from 0.2 to 2
- kinetics: float32 [8, 8], replicated, may hold values from -2 to 2
- photolysis: float32 [8], replicated, may hold values from -1 to 1
- heat_weights: float32 [3, 8], replicated, may hold values from -2 to 2
Outputs:
- tracers_out: float32 [8, 8, 384, 4096], P(None, 'lev', ('wave', 'grp'))
- heating_spectra: float32 [2, 3, 8, 96, 1024], P(None, None, 'lev', ('wave', 'grp'))
Inputs may be any that keep to these rules, and one draw needn't show every extreme that they name: `wavenumbers`: ascending and distinct; slot s holds a value from s * (10) to (s + 1) * 10 - 1.
All inputs are finite; a program needn't handle non-finite values.
Results may differ from a plain program's by a relative error of at most 0.0025.
Values sent between devices are 32-bit elements; how exact they have to be, the bound alone decides.
A program may use at most 32 MiB of HBM per device.

v0:
```python
import math

import jax
import jax.numpy as jnp
from jax import lax
from jax.sharding import PartitionSpec as P

NLON = 4096


highest = lax.Precision.HIGHEST


def sent_to_all(x, axis):
    length = lax.axis_size(axis)
    return lax.all_to_all(jnp.broadcast_to(x[None], (length, *x.shape)), axis, 0, 0, tiled=True)


def laid_out(tiles, dim):
    dims = list(tiles.shape[1:])
    dims[dim] *= tiles.shape[0]
    return jnp.moveaxis(tiles, 0, dim).reshape(dims)


def gather_directly(x, axis, dim):
    tiles = sent_to_all(x, axis)
    return laid_out(tiles, dim)


def with_halo(x, sides, width):
    edges = {}
    for axis, dim in sides:
        size, length = (lax.axis_size(axis), x.shape[dim])
        up = [(i, (i + 1) % size) for i in range(size - 1)]
        last = lax.slice_in_dim(x, length - width, length, axis=dim)
        first = lax.slice_in_dim(x, 0, width, axis=dim)
        edges[dim] = (
            lax.ppermute(last, axis, up),
            lax.ppermute(first, axis, [(b, a) for a, b in up]),
        )
    done = []
    for _, dim in sides:
        low, high = edges[dim]
        around = [(width, width) if d in done else (0, 0) for d in range(x.ndim)]
        x = jnp.concatenate([jnp.pad(low, around), x, jnp.pad(high, around)], axis=dim)
        done.append(dim)
    return x


def fourier_table(wavenumbers):
    longitudes = jnp.arange(NLON, dtype=jnp.int32)
    phase_index = wavenumbers[:, None] * longitudes[None, :] % NLON
    angles = phase_index.astype(jnp.float32) * (2.0 * math.pi / NLON)
    return jnp.stack([jnp.cos(angles), -jnp.sin(angles)])


def advect(padded, courant_x, courant_y):
    centre = padded[..., 1:-1, :]
    northern = padded[..., :-2, :]
    southern = padded[..., 2:, :]
    western = jnp.roll(centre, 1, axis=-1)
    eastern = jnp.roll(centre, -1, axis=-1)
    return (
        centre
        - jnp.maximum(courant_x, 0.0) * (centre - western)
        - jnp.minimum(courant_x, 0.0) * (eastern - centre)
        - jnp.maximum(courant_y, 0.0) * (centre - northern)
        - jnp.minimum(courant_y, 0.0) * (southern - centre)
    )


def react(tracer_now, react_rate, photo_rate, kinetics, photolysis):
    mixed = jnp.tensordot(kinetics, tracer_now, axes=1, precision=highest)
    yields = photolysis.reshape((-1,) + (1,) * (tracer_now.ndim - 1))
    return tracer_now + 0.2 * react_rate * mixed + 0.2 * photo_rate * yields * tracer_now[0]


def body(spectra, legendre, wavenumbers, quad_weights, tracers, kinetics, photolysis, heat_weights):
    local_count = legendre.shape[0]
    ndegree = legendre.shape[1]
    position = lax.axis_index(("wave", "grp"))
    own_waves = lax.dynamic_slice_in_dim(wavenumbers, position * local_count, local_count)
    degree_mask = jnp.arange(ndegree, dtype=jnp.int32)[None, :] < (ndegree - own_waves)[:, None]
    masked_coeffs = jnp.where(degree_mask, spectra[:, :, 0], jnp.zeros((), spectra.dtype))
    fourier = jnp.einsum(
        "pfsj,sjy->pfsy", masked_coeffs, legendre, preferred_element_type=jnp.float32
    )
    total_waves = wavenumbers.shape[0]
    shared_table = fourier_table(wavenumbers)
    synth_scale = 1.0 / math.sqrt(total_waves)
    grid_fields = (
        jnp.einsum(
            "pksy,psx->kyx",
            lax.all_to_all(fourier, ("wave", "grp"), split_axis=3, concat_axis=2, tiled=True),
            shared_table,
            precision=highest,
        )
        * synth_scale
    )
    courant_x = 0.45 * jnp.tanh(grid_fields[0])
    courant_y = 0.45 * jnp.tanh(grid_fields[1])
    react_rate = jnp.exp(0.3 * grid_fields[2])
    tracer_now = tracers[:, 0]
    levels = lax.axis_size("lev")
    my_level = lax.axis_index("lev")
    block_in = gather_directly(tracer_now[0][None], "lev", 0)
    level_ids = jnp.arange(block_in.shape[0], dtype=jnp.int32)
    chosen = (level_ids < my_level).astype(jnp.float32)
    overhead = jnp.sum(chosen[:, None, None] * block_in, axis=0)
    photo_rate = jnp.exp(-2.0 * overhead / levels)
    for substep in range(2):
        padded = with_halo(tracer_now, ((("wave", "grp"), 1),), 1)
        tracer_now = react(
            advect(padded, courant_x, courant_y), react_rate, photo_rate, kinetics, photolysis
        )
    heating = jnp.tensordot(heat_weights, tracer_now, axes=1, precision=highest) * (
        1.0 + 0.5 * jnp.tanh(grid_fields[3])
    )
    heat_fourier = jnp.einsum("kyx,psx->pksy", heating, shared_table, precision=highest) * (
        1.0 / math.sqrt(NLON)
    )
    weighted = (
        lax.all_to_all(heat_fourier, ("wave", "grp"), split_axis=2, concat_axis=3, tiled=True)
        * quad_weights
    ).astype(jnp.bfloat16)
    heating_spectra = jnp.einsum(
        "pksy,sjy->pksj", weighted, legendre, preferred_element_type=jnp.float32
    )
    heating_spectra = jnp.where(degree_mask, heating_spectra, jnp.zeros((), jnp.float32))
    return (tracer_now[:, None], heating_spectra[:, :, None])


def solution(mesh):
    return jax.shard_map(
        body,
        mesh=mesh,
        in_specs=(
            P(None, None, "lev", ("wave", "grp"), None),
            P(("wave", "grp"), None, None),
            P(),
            P(),
            P(None, "lev", ("wave", "grp"), None),
            P(),
            P(),
            P(),
        ),
        out_specs=(
            P(None, "lev", ("wave", "grp"), None),
            P(None, None, "lev", ("wave", "grp"), None),
        ),
        check_vma=False,
    )
```

profile of v0, /device:TPU:1, one launch (start us, length us, event | category | flops | bytes accessed | tf_op | source)
XLA Modules:
  0.0 122.3 jit_solution(16233038133022540111)
XLA Ops:
  0.6 0.0 copy-start
  0.6 0.0 copy-start.4
  0.7 1.3 %dynamic_slice.3 = s32[1]{0:T(128)} dynamic-slice(s32[96]{0:T(128)} %param.10, s32[]{:T(128)S(6)} %select_n.38), dynamic_slice_sizes={1} | dynamic-slice | bytes 12 | tf_op jit(solution)/shard_map/dynamic_slice | solution.py:82
  2.7 0.9 convolution_bitcast_fusion.2
  3.6 0.9 copy.42
  4.6 20.0 %all-to-all-start = ((f32[2,4,1,384]{1,0,2,3:T(2,128)}), f32[2,4,1,384]{1,0,2,3:T(2,128)S(1)}, u32[]{:S(2)}, u32[]{:S(2)}) async-start(f32[2,4,1,384]{1,0,2,3:T(2,128)} %copy.42), calls=%async_computation | async-start | bytes 786432 | tf_op jit(solution)/shard_map/all_to_all | solution.py:94
  24.6 0.3 copy.69
  24.9 0.7 fusion.68
  25.6 3.5 %collective-permute-start = (f32[8,1,4096]{2,0,1:T(8,128)}, f32[8,1,4096]{2,0,1:T(8,128)}, u32[]{:S(2)}, u32[]{:S(2)}) collective-permute-start(f32[8,1,4096]{2,0,1:T(8,128)} %get-tuple-element.22), channel_id=1, source_target_pairs={{0,1},{1,2},{2,3},{3,4},{4,5},{5,6},{6,7},{7,64},{64,65},{65,66},{... | collective-permute-start | bytes 393224 | tf_op jit(solution)/shard_map/ppermute | solution.py:38
  29.1 1.9 %collective-permute-start.1 = (f32[8,1,4096]{2,0,1:T(8,128)S(1)}, f32[8,1,4096]{2,0,1:T(8,128)}, u32[]{:S(2)}, u32[]{:S(2)}) collective-permute-start(f32[8,1,4096]{2,0,1:T(8,128)S(1)} %get-tuple-element.23), channel_id=1, source_target_pairs={{1,0},{2,1},{3,2},{4,3},{5,4},{6,5},{7,6},{64,7},{65,64},{66,65},{... | collective-permute-start | bytes 393224 | tf_op jit(solution)/shard_map/ppermute | solution.py:39
  31.1 7.4 %fusion.21 = (f32[1,96,4096]{2,1,0:T(8,128)S(1)}, f32[1,96,4096]{2,1,0:T(8,128)}) fusion(s32[96]{0:T(128)S(1)} %copy-done.19), kind=kLoop, calls=%fused_computation.32 | loop fusion | flops 5898240 | bytes 3146112 | tf_op jit(solution)/shard_map/cos | solution.py:54
  38.5 1.1 fusion.66
  39.6 0.7 fusion.67
  40.3 0.8 slice_bitcast_fusion
  41.2 0.6 compare_convert_fusion
  41.7 4.4 %all-to-all-done = f32[2,4,1,384]{1,0,2,3:T(2,128)S(1)} async-done(((f32[2,4,1,384]{1,0,2,3:T(2,128)}), f32[2,4,1,384]{1,0,2,3:T(2,128)S(1)}, u32[]{:S(2)}, u32[]{:S(2)}) %all-to-all-start) | async-done | bytes 12320 | tf_op jit(solution)/shard_map/all_to_all | solution.py:94
  46.1 0.9 broadcast_in_dim.25
  47.0 6.8 %all-to-all-start.1 = ((f32[8,1,4,4096]{3,2,1,0:T(4,128)}), f32[8,1,4,4096]{3,2,1,0:T(4,128)}, u32[]{:S(2)}, u32[]{:S(2)}) async-start(f32[8,1,4,4096]{3,2,1,0:T(4,128)} %broadcast_in_dim.25), calls=%async_computation.1 | async-start | bytes 1048576 | tf_op jit(solution)/shard_map/all_to_all | solution.py:16
  53.8 2.2 %copy.53 = f32[2,4,96,4]{3,2,1,0:T(8,128)} copy(f32[2,4,96,4]{1,0,3,2:T(2,128)S(1)} %bitcast.110) | data formatting | bytes 24576 | tf_op jit(solution)/shard_map/all_to_all | solution.py:94
  56.0 3.6 %fusion.7 = f32[4,4,4096]{2,1,0:T(4,128)S(1)} fusion(f32[2,4,96,4]{3,2,1,0:T(8,128)} %copy.53, f32[1,96,4096]{2,1,0:T(8,128)} %get-tuple-element.31, f32[1,96,4096]{2,1,0:T(8,128)S(1)} %get-tuple-element.30), kind=kOutput, calls=%fused_computation.11 | convolution fusion | flops 151846912 | bytes 3420160 | tf_op jit(solution)/shard_map/pksy,psx->kyx/dot_general | solution.py:92
  59.6 0.7 fusion.47
  60.4 1.3 %fusion.30 = f32[8,4,4096]{2,0,1:T(8,128)S(1)} fusion(f32[8,4,4096]{2,0,1:T(8,128)S(1)} %bitcast.108, f32[8,1,4096]{2,0,1:T(8,128)} %collective-permute-done.1, f32[8,1,4096]{2,0,1:T(8,128)} %collective-permute-done, f32[8,4,4095]{2,0,1:T(8,128)S(1)} %copy-done.3, f32[8,4,1]{2,0,1:T(8,128)S(1)} %copy-done.12, f32[8,4,1]{2,0,1:T(8,128)S(1)} %get-tuple-element.20, ...), kind=kLoop, calls=%fused_computation.46 | loop fusion | flops 2097152 | bytes 2621440 | tf_op jit(solution)/shard_map/sub | solution.py:64
  61.9 8.0 %all-to-all-done.1 = f32[8,1,4,4096]{3,2,1,0:T(4,128)} async-done(((f32[8,1,4,4096]{3,2,1,0:T(4,128)}), f32[8,1,4,4096]{3,2,1,0:T(4,128)}, u32[]{:S(2)}, u32[]{:S(2)}) %all-to-all-start.1) | async-done | bytes 524320 | tf_op jit(solution)/shard_map/all_to_all | solution.py:16
  69.9 1.2 %fusion.42 = f32[4,4096]{1,0:T(4,128)S(1)} fusion(f32[8,1,4,4096]{3,2,1,0:T(4,128)} %all-to-all-done.1, f32[8]{0:T(128)} %compare_convert_fusion), kind=kLoop, calls=%fused_computation.64 | loop fusion | flops 245760 | bytes 589856 | tf_op jit(solution)/shard_map/reduce_sum | solution.py:109
  71.2 1.3 %fusion.5 = f32[8,4,4096]{2,0,1:T(8,128)S(1)} fusion(f32[8,4,4096]{2,0,1:T(8,128)S(1)} %fusion.30, f32[4,4096]{1,0:T(4,128)S(1)} %bitcast.111, f32[8]{0:T(128)} %param.14, f32[4,4096]{1,0:T(4,128)S(1)} %exponential_multiply_fusion, f32[4,4096]{1,0:T(4,128)S(1)} %get-tuple-element.27, f32[8,8]{1,0:T(8,128)} %param.13), kind=kOutput, calls=%fused_computation.7 | convolution fusion | flops 13238272 | bytes 1245472 | tf_op jit(solution)/shard_map/dot_general | solution.py:73
  72.5 0.2 fusion.63
  72.8 0.0 copy-start.13
  72.8 0.0 copy-start.17
  72.8 4.6 %collective-permute-start.2 = (f32[8,1,4096]{2,0,1:T(8,128)S(1)}, f32[8,1,4096]{2,0,1:T(8,128)S(1)}, u32[]{:S(2)}, u32[]{:S(2)}) collective-permute-start(f32[8,1,4096]{2,0,1:T(8,128)S(1)} %get-tuple-element.16), channel_id=1, source_target_pairs={{0,1},{1,2},{2,3},{3,4},{4,5},{5,6},{6,7},{7,64},{64,65},{65,66},{... | collective-permute-start | bytes 393224 | tf_op jit(solution)/shard_map/ppermute | solution.py:38
  77.4 2.1 %collective-permute-start.3 = (f32[8,1,4096]{2,0,1:T(8,128)S(1)}, f32[8,1,4096]{2,0,1:T(8,128)S(1)}, u32[]{:S(2)}, u32[]{:S(2)}) collective-permute-start(f32[8,1,4096]{2,0,1:T(8,128)S(1)} %get-tuple-element.17), channel_id=1, source_target_pairs={{1,0},{2,1},{3,2},{4,3},{5,4},{6,5},{7,6},{64,7},{65,64},{66,65},{... | collective-permute-start | bytes 393224 | tf_op jit(solution)/shard_map/ppermute | solution.py:39
  79.5 0.1 fusion.64
  79.6 4.1 %collective-permute-done.3 = f32[8,1,4096]{2,0,1:T(8,128)S(1)} collective-permute-done((f32[8,1,4096]{2,0,1:T(8,128)S(1)}, f32[8,1,4096]{2,0,1:T(8,128)S(1)}, u32[]{:S(2)}, u32[]{:S(2)}) %collective-permute-start.3) | collective-permute-done | bytes 131104 | tf_op jit(solution)/shard_map/ppermute | solution.py:39
  83.8 0.3 fusion.24
  84.2 0.6 fusion.2
  84.9 0.6 fusion.6
  85.5 0.0 copy-done.1
  85.5 3.0 %fusion.18 = f32[2,3,96,4]{2,3,1,0:T(4,128)S(1)} fusion(f32[1,96,4096]{2,1,0:T(8,128)S(1)} %copy-done.1, f32[1,96,4096]{2,1,0:T(8,128)S(1)} %get-tuple-element.30, f32[3,4,4096]{2,0,1:T(4,128)S(1)} %fusion.6), kind=kOutput, calls=%fused_computation.28 | convolution fusion | flops 114034944 | bytes 3351552 | tf_op jit(solution)/shard_map/kyx,psx->pksy/dot_general | solution.py:119
  88.5 0.9 copy.46
  89.4 12.3 %all-to-all-start.2 = ((f32[2,3,96,4]{3,0,1,2:T(2,128)}), f32[2,3,96,4]{3,0,1,2:T(2,128)S(1)}, u32[]{:S(2)}, u32[]{:S(2)}) async-start(f32[2,3,96,4]{3,0,1,2:T(2,128)} %copy.46), calls=%async_computation.2 | async-start | bytes 589824 | tf_op jit(solution)/shard_map/all_to_all | solution.py:123
  101.7 0.1 mul.317
  101.8 0.1 copy.47
  101.9 1.1 copy.51
  103.0 17.7 %all-to-all-done.2 = f32[2,3,96,4]{3,0,1,2:T(2,128)S(1)} async-done(((f32[2,3,96,4]{3,0,1,2:T(2,128)}), f32[2,3,96,4]{3,0,1,2:T(2,128)S(1)}, u32[]{:S(2)}, u32[]{:S(2)}) %all-to-all-start.2) | async-done | bytes 9248 | tf_op jit(solution)/shard_map/all_to_all | solution.py:123
  120.7 0.2 copy.48
  120.9 0.2 copy.58
  121.1 0.2 reshape.171
  121.3 0.3 fusion.16
  121.6 0.7 copy.52
  (46 shorter events, 0.3 us)
Async XLA Ops:
  0.6 2.0 %copy-start = (bf16[1,1024,384]{2,1,0:T(8,128)(2,1)S(1)}, bf16[1,1024,384]{2,1,0:T(8,128)(2,1)}, u32[]{:S(2)}) copy-start(bf16[1,1024,384]{2,1,0:T(8,128)(2,1)} %param.9) | copy-start | bytes 2359300
  0.6 24.0 %copy-start.4 = (f32[8,1,4,4096]{3,2,1,0:T(4,128)S(1)}, f32[8,1,4,4096]{3,2,1,0:T(4,128)}, u32[]{:S(2)}) copy-start(f32[8,1,4,4096]{3,2,1,0:T(4,128)} %param.12) | copy-start | bytes 1572868
  2.7 22.9 %copy-start.14 = (pred[1024]{0:T(1024)(128)(4,1)}, pred[1024]{0:T(1024)(128)(4,1)S(1)}, u32[]{:S(2)}) copy-start(pred[1024]{0:T(1024)(128)(4,1)S(1)} %iota_compare_fusion) | copy-start | bytes 3076
  3.6 27.4 %copy-start.19 = (s32[96]{0:T(128)S(1)}, s32[96]{0:T(128)}, u32[]{:S(2)}) copy-start(s32[96]{0:T(128)} %param.10) | copy-start | bytes 1156
  4.6 41.5 %all-to-all-start = ((f32[2,4,1,384]{1,0,2,3:T(2,128)}), f32[2,4,1,384]{1,0,2,3:T(2,128)S(1)}, u32[]{:S(2)}, u32[]{:S(2)}) async-start(f32[2,4,1,384]{1,0,2,3:T(2,128)} %copy.42), calls=%async_computation | async-start | bytes 786432 | tf_op jit(solution)/shard_map/all_to_all | solution.py:94
  25.6 34.7 %collective-permute-start = (f32[8,1,4096]{2,0,1:T(8,128)}, f32[8,1,4096]{2,0,1:T(8,128)}, u32[]{:S(2)}, u32[]{:S(2)}) collective-permute-start(f32[8,1,4096]{2,0,1:T(8,128)} %get-tuple-element.22), channel_id=1, source_target_pairs={{0,1},{1,2},{2,3},{3,4},{4,5},{5,6},{6,7},{7,64},{64,65},{65,66},{... | collective-permute-start | bytes 393224 | tf_op jit(solution)/shard_map/ppermute | solution.py:38
  29.1 31.2 %collective-permute-start.1 = (f32[8,1,4096]{2,0,1:T(8,128)S(1)}, f32[8,1,4096]{2,0,1:T(8,128)}, u32[]{:S(2)}, u32[]{:S(2)}) collective-permute-start(f32[8,1,4096]{2,0,1:T(8,128)S(1)} %get-tuple-element.23), channel_id=1, source_target_pairs={{1,0},{2,1},{3,2},{4,3},{5,4},{6,5},{7,6},{64,7},{65,64},{66,65},{... | collective-permute-start | bytes 393224 | tf_op jit(solution)/shard_map/ppermute | solution.py:39
  47.0 22.9 %all-to-all-start.1 = ((f32[8,1,4,4096]{3,2,1,0:T(4,128)}), f32[8,1,4,4096]{3,2,1,0:T(4,128)}, u32[]{:S(2)}, u32[]{:S(2)}) async-start(f32[8,1,4,4096]{3,2,1,0:T(4,128)} %broadcast_in_dim.25), calls=%async_computation.1 | async-start | bytes 1048576 | tf_op jit(solution)/shard_map/all_to_all | solution.py:16
  56.0 4.4 %copy-start.2 = (f32[8,4,4095]{2,0,1:T(8,128)S(1)}, f32[8,4,4095]{2,0,1:T(8,128)}, u32[]{:S(2)}) copy-start(f32[8,4,4095]{2,0,1:T(8,128)} %get-tuple-element.18) | copy-start | bytes 1572484
  56.0 4.4 %copy-start.3 = (f32[8,4,4095]{2,0,1:T(8,128)S(1)}, f32[8,4,4095]{2,0,1:T(8,128)}, u32[]{:S(2)}) copy-start(f32[8,4,4095]{2,0,1:T(8,128)} %get-tuple-element.19) | copy-start | bytes 1572484
  56.0 4.4 %copy-start.12 = (f32[8,4,1]{2,0,1:T(8,128)S(1)}, f32[8,4,1]{2,0,1:T(8,128)}, u32[]{:S(2)}) copy-start(f32[8,4,1]{2,0,1:T(8,128)} %get-tuple-element.21) | copy-start | bytes 388
  60.3 1.4 %copy-start.5 = (f32[4,4096]{1,0:T(4,128)}, f32[4,4096]{1,0:T(4,128)S(1)}, u32[]{:S(2)}) copy-start(f32[4,4096]{1,0:T(4,128)S(1)} %get-tuple-element.26) | copy-start | bytes 196612
  60.3 1.4 %copy-start.7 = (f32[4,4096]{1,0:T(4,128)}, f32[4,4096]{1,0:T(4,128)S(1)}, u32[]{:S(2)}) copy-start(f32[4,4096]{1,0:T(4,128)S(1)} %get-tuple-element.28) | copy-start | bytes 196612
  60.3 1.4 %copy-start.9 = (f32[4,4096]{1,0:T(4,128)}, f32[4,4096]{1,0:T(4,128)S(1)}, u32[]{:S(2)}) copy-start(f32[4,4096]{1,0:T(4,128)S(1)} %get-tuple-element.29) | copy-start | bytes 196612
  72.5 11.2 %copy-start.6 = (f32[4,4096]{1,0:T(4,128)S(1)}, f32[4,4096]{1,0:T(4,128)}, u32[]{:S(2)}) copy-start(f32[4,4096]{1,0:T(4,128)} %copy-done.5) | copy-start | bytes 196612
  72.5 11.2 %copy-start.8 = (f32[4,4096]{1,0:T(4,128)S(1)}, f32[4,4096]{1,0:T(4,128)}, u32[]{:S(2)}) copy-start(f32[4,4096]{1,0:T(4,128)} %copy-done.7) | copy-start | bytes 196612
  72.5 11.2 %copy-start.10 = (f32[4,4096]{1,0:T(4,128)S(1)}, f32[4,4096]{1,0:T(4,128)}, u32[]{:S(2)}) copy-start(f32[4,4096]{1,0:T(4,128)} %copy-done.9) | copy-start | bytes 196612
  72.8 11.4 %copy-start.13 = (f32[8,8]{1,0:T(8,128)S(1)}, f32[8,8]{1,0:T(8,128)}, u32[]{:S(2)}) copy-start(f32[8,8]{1,0:T(8,128)} %param.13) | copy-start | bytes 772
  72.8 11.4 %copy-start.17 = (f32[8]{0:T(128)S(1)}, f32[8]{0:T(128)}, u32[]{:S(2)}) copy-start(f32[8]{0:T(128)} %param.14) | copy-start | bytes 100
  72.8 6.8 %collective-permute-start.2 = (f32[8,1,4096]{2,0,1:T(8,128)S(1)}, f32[8,1,4096]{2,0,1:T(8,128)S(1)}, u32[]{:S(2)}, u32[]{:S(2)}) collective-permute-start(f32[8,1,4096]{2,0,1:T(8,128)S(1)} %get-tuple-element.16), channel_id=1, source_target_pairs={{0,1},{1,2},{2,3},{3,4},{4,5},{5,6},{6,7},{7,64},{64,65},{65,66},{... | collective-permute-start | bytes 393224 | tf_op jit(solution)/shard_map/ppermute | solution.py:38
  77.4 6.3 %collective-permute-start.3 = (f32[8,1,4096]{2,0,1:T(8,128)S(1)}, f32[8,1,4096]{2,0,1:T(8,128)S(1)}, u32[]{:S(2)}, u32[]{:S(2)}) collective-permute-start(f32[8,1,4096]{2,0,1:T(8,128)S(1)} %get-tuple-element.17), channel_id=1, source_target_pairs={{1,0},{2,1},{3,2},{4,3},{5,4},{6,5},{7,6},{64,7},{65,64},{66,65},{... | collective-permute-start | bytes 393224 | tf_op jit(solution)/shard_map/ppermute | solution.py:39
  83.7 1.1 copy-start.11
  83.7 1.1 copy-start.16
  84.1 1.4 %copy-start.1 = (f32[1,96,4096]{2,1,0:T(8,128)S(1)}, f32[1,96,4096]{2,1,0:T(8,128)}, u32[]{:S(2)}) copy-start(f32[1,96,4096]{2,1,0:T(8,128)} %get-tuple-element.31) | copy-start | bytes 4718596
  85.5 16.2 %copy-start.18 = (f32[384]{0:T(512)S(1)}, f32[384]{0:T(512)}, u32[]{:S(2)}) copy-start(f32[384]{0:T(512)} %param.11) | copy-start | bytes 4612
  88.5 32.8 %copy-start.15 = (pred[1024]{0:T(1024)(128)(4,1)S(1)}, pred[1024]{0:T(1024)(128)(4,1)}, u32[]{:S(2)}) copy-start(pred[1024]{0:T(1024)(128)(4,1)} %copy-done.14) | copy-start | bytes 3076
  89.4 31.3 %all-to-all-start.2 = ((f32[2,3,96,4]{3,0,1,2:T(2,128)}), f32[2,3,96,4]{3,0,1,2:T(2,128)S(1)}, u32[]{:S(2)}, u32[]{:S(2)}) async-start(f32[2,3,96,4]{3,0,1,2:T(2,128)} %copy.46), calls=%async_computation.2 | async-start | bytes 589824 | tf_op jit(solution)/shard_map/all_to_all | solution.py:123
where the time goes:
time: 123 us; the launch traced here: 122 us
  starting transfers between devices  51.3 us (42%)
  waiting for transfers between devices  34.2 us (28%)
  local copies, waits for them, and re-layouts  12.9 us (10%)
  other arithmetic  11.7 us (10%)
  matrix products  10.4 us (8%)
  between operations  1.72 us (1%)
    all_to_all x1, starting transfers between devices, body(): lax.all_to_all(fourier, ('wave', 'grp'), split_axis=3, concat_axis=2, til...  20 us
    all_to_all x1, waiting for transfers between devices, body(): lax.all_to_all(heat_fourier, ('wave', 'grp'), split_axis=2, concat_axis=3...  17.7 us
    all_to_all x1, starting transfers between devices, body(): lax.all_to_all(heat_fourier, ('wave', 'grp'), split_axis=2, concat_axis=3...  12.3 us
    ppermute x2, starting transfers between devices, with_halo(): lax.ppermute(last, axis, up)  8.18 us
    all_to_all x1, waiting for transfers between devices, sent_to_all(): lax.all_to_all(jnp.broadcast_to(x[None], (length, *x.shape)), axis, 0, 0,...  8.03 us
    cos x1, other arithmetic, fourier_table(): return jnp.stack([jnp.cos(angles), -jnp.sin(angles)])  7.45 us
    all_to_all x1, starting transfers between devices, sent_to_all(): lax.all_to_all(jnp.broadcast_to(x[None], (length, *x.shape)), axis, 0, 0,...  6.82 us
    all_to_all x1, waiting for transfers between devices, body(): lax.all_to_all(fourier, ('wave', 'grp'), split_axis=3, concat_axis=2, til...  4.36 us
  transfers between devices with their start and end apart: 7, of which 4 were waited for; matrix products, arithmetic and copies ran while one was open for 18% of the time, Pallas kernels for 0%

commit v1 on v0

v1 whole, which is shorter than its diff:
```python
import math

import jax
import jax.numpy as jnp
from jax import lax
from jax.experimental import pallas as pl
from jax.experimental.pallas import tpu as pltpu
from jax.sharding import PartitionSpec as P

NW, NL, NG = 12, 8, 8
NPOS = NW * NG
NDEG = 1024
NLON = 4096
NLAT = 384
CHUNK = NLON // NL
F32 = jnp.float32
BF16 = jnp.bfloat16
MESH = pl.DeviceIdType.MESH
NT = (((1,), (1,)), ((), ()))
FAR_W = (6, 5, 7, 4, 8, 3, 9, 2, 10, 1, 11)
FAR_G = (4, 3, 5, 2, 6, 7, 1)
FAR_L = (4, 3, 5, 2, 6, 1, 7)


def cos_sin(m):
    shifted = m + NLON // 8
    quarter = (shifted >> 10) & 3
    angle = ((shifted & (NLON // 4 - 1)) - NLON // 8).astype(F32) * (2.0 * math.pi / NLON)
    z = angle * angle
    s = angle * (1.0 + z * (-1.0 / 6 + z * (1.0 / 120 + z * (-1.0 / 5040 + z * (1.0 / 362880)))))
    c = 1.0 + z * (-0.5 + z * (1.0 / 24 + z * (-1.0 / 720 + z * (1.0 / 40320))))
    odd = (quarter & 1) == 1
    cos = jnp.where(odd, s, c)
    sin = jnp.where(odd, c, s)
    cos = jnp.where(((quarter + 1) & 2) == 2, -cos, cos)
    sin = jnp.where((quarter & 2) == 2, -sin, sin)
    return cos, sin


def split(x):
    hi = x.astype(BF16)
    return hi, (x - hi.astype(F32)).astype(BF16)


def dot3(x, bh, bl, dims):
    hi, lo = split(x)
    out = lax.dot_general(hi, bh, dims, preferred_element_type=F32)
    out += lax.dot_general(lo, bh, dims, preferred_element_type=F32)
    return out + lax.dot_general(hi, bl, dims, preferred_element_type=F32)


def kernel(
    spec, leg, wn, quad, trc, kin, pho, hw,
    tout, sout,
    C, D, O, LV, X, T, S, Z1, G1, V, LR, PC, PH, COEF, AT, BH, BL, H, HF, S2, Z2, G2, WT, WC,
    local, zs, zr, gs, gr, ls, lr, ps, pr, es, er, hs, hr, zs2, zr2, gs2, gr2,
):
    w = lax.axis_index("wave")
    l = lax.axis_index("lev")
    g = lax.axis_index("grp")
    pos = w * NG + g
    up = lax.rem(pos + 1, NPOS)
    down = lax.rem(pos + NPOS - 1, NPOS)
    up_w, up_g = up // NG, lax.rem(up, NG)
    down_w, down_g = down // NG, lax.rem(down, NG)

    for i in range(4):
        rows = pl.ds(256 * i, 256)
        pltpu.make_async_copy(leg.at[0, rows, :], LV.at[rows, :], local.at[i]).start()
    own_rows = pltpu.make_async_copy(trc.at[:, 0], C.at[:, pl.ds(2, 4), :], local.at[4])
    own_rows.start()
    PH[...] = jnp.zeros_like(PH)

    barrier = pltpu.get_barrier_semaphore()

    def hello(dw, dl, dg):
        pl.semaphore_signal(barrier, inc=1, device_id=(dw, dl, dg), device_id_type=MESH)

    for k in FAR_W:
        hello(lax.rem(w + k, NW), l, g)
    for k in range(NL):
        ll = lax.rem(l + k, NL)
        hello(up_w, ll, up_g)
        hello(down_w, ll, down_g)
        if k:
            hello(w, ll, g)
    for k in FAR_G:
        hello(w, l, lax.rem(g + k, NG))
    count = (NW - 1) + (NG - 1) + (NL - 1) + 2 * NL

    own_wave = wn[pos]
    for p in range(2):
        for f in range(4):
            X[pl.ds(4 * p + f, 1), :] = spec[p, f, 0].astype(F32)
    degree = lax.broadcasted_iota(jnp.int32, (8, NDEG), 1)
    coeffs = jnp.where(degree < NDEG - own_wave, X[...], 0.0).astype(BF16)
    fourier = jnp.zeros((8, NLAT), F32)
    for i in range(4):
        rows = pl.ds(256 * i, 256)
        pltpu.make_async_copy(leg.at[0, rows, :], LV.at[rows, :], local.at[i]).wait()
        fourier += jnp.dot(
            coeffs[:, 256 * i : 256 * i + 256], LV[rows, :], preferred_element_type=F32
        )
    groups = []
    for c in range(2):
        for r in range(8):
            shift = (NLAT - (4 * c + r - 2)) % NLAT
            groups.append(pltpu.roll(fourier, shift, 1) if shift else fourier)
    T[...] = jnp.concatenate(groups, axis=0).T
    S[...] = T[pl.ds(0, 48, stride=8), :].reshape(NW, 4, 128)
    own_rows.wait()

    pl.semaphore_wait(barrier, count)

    def z_copy(src, dst, ssem, rsem, k):
        there = lax.rem(w + k, NW)
        return pltpu.make_async_remote_copy(
            src.at[there], dst.at[w], ssem.at[k], rsem.at[w],
            device_id=(there, l, g), device_id_type=MESH,
        )

    def z_arrival(src, dst, ssem, rsem, k):
        there = lax.rem(w + k, NW)
        return pltpu.make_async_remote_copy(
            src.at[there], dst.at[there], ssem.at[k], rsem.at[there],
            device_id=(there, l, g), device_id_type=MESH,
        )

    def g_copy(src, dst, ssem, rsem, k, share):
        there = lax.rem(g + k, NG)
        return pltpu.make_async_remote_copy(
            src.at[:, there // share, :], dst.at[:, g, :], ssem.at[k], rsem.at[g],
            device_id=(w, l, there), device_id_type=MESH,
        )

    def g_arrival(src, dst, ssem, rsem, k, share):
        there = lax.rem(g + k, NG)
        return pltpu.make_async_remote_copy(
            src.at[:, there // share, :], dst.at[:, there, :], ssem.at[k], rsem.at[there],
            device_id=(w, l, there), device_id_type=MESH,
        )

    def l_copy(k, arrival=False):
        there = lax.rem(l + k, NL)
        return pltpu.make_async_remote_copy(
            C.at[0, pl.ds(2, 4), pl.ds(pl.multiple_of(CHUNK * there, CHUNK), CHUNK)],
            LR.at[there if arrival else l], ls.at[k], lr.at[there if arrival else l],
            device_id=(w, there, g), device_id_type=MESH,
        )

    def p_copy(k, arrival=False):
        there = lax.rem(l + k, NL)
        part = there if arrival else l
        return pltpu.make_async_remote_copy(
            PC.at[there],
            PH.at[pl.ds(2, 4), pl.ds(pl.multiple_of(CHUNK * part, CHUNK), CHUNK)],
            ps.at[k], pr.at[part],
            device_id=(w, there, g), device_id_type=MESH,
        )

    def e_copy(side, k, arrival=False):
        there = lax.rem(l + k, NL)
        part = there if arrival else l
        return pltpu.make_async_remote_copy(
            PC.at[there, pl.ds(3 if side else 0, 1)],
            PH.at[pl.ds(1 if side else 6, 1), pl.ds(pl.multiple_of(CHUNK * part, CHUNK), CHUNK)],
            es.at[side, k], er.at[side, part],
            device_id=(up_w, there, up_g) if side else (down_w, there, down_g),
            device_id_type=MESH,
        )

    def h_copy(side):
        return pltpu.make_async_remote_copy(
            C.at[:, pl.ds(4 if side else 2, 2), :],
            C.at[:, pl.ds(0 if side else 6, 2), :],
            hs.at[side], hr.at[side],
            device_id=(up_w, l, up_g) if side else (down_w, l, down_g),
            device_id_type=MESH,
        )

    for k in FAR_W:
        z_copy(S, Z1, zs, zr, k).start()
    for k in FAR_L:
        l_copy(k).start()
    for side in range(2):
        h_copy(side).start()
    Z1[w] = S[w]
    LR[l] = C[0, pl.ds(2, 4), pl.ds(pl.multiple_of(CHUNK * l, CHUNK), CHUNK)]

    for s in range(NPOS):
        WC[pl.ds(s, 1), :] = jnp.full((1, 128), wn[s], jnp.int32)
    WC[pl.ds(NPOS, 128 - NPOS), :] = jnp.zeros((128 - NPOS, 128), jnp.int32)
    waves = WC[...]
    across = waves.astype(F32).T[:16, :].astype(jnp.int32)
    coarse = lax.broadcasted_iota(jnp.int32, (16, 128), 0) * 256
    AT[0], AT[1] = cos_sin((across * coarse) & (NLON - 1))
    used = lax.broadcasted_iota(jnp.int32, (128, 128), 0) < NPOS
    for half in range(2):
        fine = lax.broadcasted_iota(jnp.int32, (128, 128), 1) + 128 * half
        cos, sin = cos_sin((waves * fine) & (NLON - 1))
        for p, table in enumerate((cos, -sin)):
            hi, lo = split(jnp.where(used, table, 0.0))
            BH[pl.ds(128 * p, 128), pl.ds(128 * half, 128)] = hi
            BL[pl.ds(128 * p, 128), pl.ds(128 * half, 128)] = lo

    for k in range(1, NL):
        l_copy(k, True).wait_recv()
    total = jnp.zeros((4, CHUNK), F32)
    for level in range(NL):
        PC[level] = 0.2 * jnp.exp(total * (-2.0 / NL))
        if level < NL - 1:
            total += LR[level]
    for k in FAR_L:
        p_copy(k).start()
    for k in range(NL):
        for side in range(2):
            e_copy(side, k).start()
    PH[pl.ds(2, 4), pl.ds(pl.multiple_of(CHUNK * l, CHUNK), CHUNK)] = PC[l]

    for k in range(1, NW):
        z_arrival(S, Z1, zs, zr, k).wait_recv()
    for k in FAR_G:
        g_copy(Z1, G1, gs, gr, k, 2).start()
    G1[:, pl.ds(g, 1), :] = Z1[:, pl.ds(g // 2, 1), :]

    for side in range(2):
        h_copy(side).wait_recv()

    @pl.when(pos == 0)
    def _():
        C[:, pl.ds(0, 2), :] = jnp.zeros((8, 2, NLON), F32)

    @pl.when(pos == NPOS - 1)
    def _():
        C[:, pl.ds(6, 2), :] = jnp.zeros((8, 2, NLON), F32)

    for k in range(1, NG):
        g_arrival(Z1, G1, gs, gr, k, 2).wait_recv()

    arrived = jnp.concatenate([G1[...].reshape(NPOS, 128), jnp.zeros((128 - NPOS, 128), F32)], axis=0)
    V[...] = arrived.T
    second = lax.rem(g, 2) == 1
    parts = []
    for p in range(2):
        fields = []
        for f in range(4):
            first = V[pl.ds(4 * p + f, 8, stride=8), :]
            other = V[pl.ds(64 + 4 * p + f, 8, stride=8), :]
            fields.append(jnp.where(second, other, first))
        parts.append(jnp.concatenate(fields, axis=0) * (1.0 / math.sqrt(NPOS)))
    real, imag = parts
    latitude = lax.broadcasted_iota(jnp.int32, (8, 256), 0) + (4 * pos - 2)
    inside = jnp.where((latitude >= 0) & (latitude < NLAT), 1.0, 0.0)
    bh, bl = BH[...], BL[...]
    for part in range(4):
        turned = []
        for i in range(4):
            h = 4 * part + i
            ca, sa = AT[0, pl.ds(h, 1), :], AT[1, pl.ds(h, 1), :]
            turned.append(
                jnp.concatenate([real * ca - imag * sa, real * sa + imag * ca], axis=1)
            )
        grid = dot3(jnp.concatenate(turned, axis=0), bh, bl, (((1,), (0,)), ((), ())))
        for i in range(4):
            cols = pl.ds(256 * (4 * part + i), 256)
            field = [grid[32 * i + 8 * f : 32 * i + 8 * f + 8, :] for f in range(4)]
            cx = 0.45 * jnp.tanh(field[0]) * inside
            cy = 0.45 * jnp.tanh(field[1]) * inside
            COEF[0, :, cols] = inside - jnp.abs(cx) - jnp.abs(cy)
            COEF[1, :, cols] = jnp.maximum(cx, 0.0)
            COEF[2, :, cols] = jnp.maximum(-cx, 0.0)
            COEF[3, :, cols] = jnp.maximum(cy, 0.0)
            COEF[4, :, cols] = jnp.maximum(-cy, 0.0)
            COEF[5, :, cols] = 0.2 * jnp.exp(0.3 * field[2])
            COEF[6, :, cols] = 1.0 + 0.5 * jnp.tanh(field[3])

    for k in range(NL):
        if k:
            p_copy(k, True).wait_recv()
        for side in range(2):
            e_copy(side, k, True).wait_recv()

    lane = lax.broadcasted_iota(jnp.int32, (8, 128), 1)

    def substep(src, dst, last):
        def block(b, carry):
            here = pl.ds(pl.multiple_of(b * 128, 128), 128)
            west = pl.ds(pl.multiple_of(lax.rem(b + 31, 32) * 128, 128), 128)
            east = pl.ds(pl.multiple_of(lax.rem(b + 1, 32) * 128, 128), 128)
            cc, xp, xm, yp, ym = [COEF[i, :, here] for i in range(5)]
            moved = []
            for t in range(8):
                c = src[t, :, here]
                western = pltpu.roll(jnp.where(lane == 127, src[t, :, west], c), 1, 1)
                eastern = pltpu.roll(jnp.where(lane == 0, src[t, :, east], c), 127, 1)
                northern = pltpu.roll(c, 1, 0)
                southern = pltpu.roll(c, 7, 0)
                moved.append(cc * c + xp * western + xm * eastern + yp * northern + ym * southern)
            rate = COEF[5, :, here]
            light = PH[:, here] * moved[0]
            done = []
            for i in range(8):
                mixed = kin[i, 0] * moved[0]
                for t in range(1, 8):
                    mixed += kin[i, t] * moved[t]
                done.append(moved[i] + rate * mixed + pho[i] * light)
                dst[i, :, here] = done[i]
            if last:
                gain = COEF[6, :, here]
                for k in range(3):
                    heat = hw[k, 0] * done[0]
                    for t in range(1, 8):
                        heat += hw[k, t] * done[t]
                    H[b, pl.ds(8 * k, 8), :] = heat * gain
            return carry

        lax.fori_loop(0, 32, block, 0, unroll=2)

    substep(C, D, False)
    substep(D, O, True)
    result = pltpu.make_async_copy(O.at[:, pl.ds(2, 4), :], tout.at[:, 0], local.at[5])
    result.start()

    zr_sum = jnp.zeros((24, 128), F32)
    zi_sum = jnp.zeros((24, 128), F32)
    for part in range(4):
        rows = []
        for i in range(4):
            h = 4 * part + i
            rows.append(jnp.concatenate([H[2 * h], H[2 * h + 1]], axis=1))
        spectrum = dot3(jnp.concatenate(rows, axis=0), bh, bl, NT)
        for i in range(4):
            h = 4 * part + i
            ca, sa = AT[0, pl.ds(h, 1), :], AT[1, pl.ds(h, 1), :]
            yc = spectrum[24 * i : 24 * i + 24, :128]
            ys = spectrum[24 * i : 24 * i + 24, 128:]
            zr_sum += ca * yc + sa * ys
            zi_sum += ca * ys - sa * yc
    scale = 1.0 / math.sqrt(NLON)
    HF[pl.ds(0, 24), :] = zr_sum * scale
    HF[pl.ds(24, 24), :] = zi_sum * scale
    HF[pl.ds(48, 16), :] = jnp.zeros((16, 128), F32)
    mine = jnp.concatenate([HF[pl.ds(r, 8, stride=8), :] for r in range(2, 6)], axis=0)
    V[...] = jnp.concatenate(
        [pltpu.roll(mine, 128 - d, 1) if d else mine for d in range(4)], axis=0
    ).T
    S2[...] = V[pl.ds(0, 24, stride=4), :].reshape(NW, 2, 128)
    for k in FAR_W:
        z_copy(S2, Z2, zs2, zr2, k).start()
    Z2[w] = S2[w]
    for k in range(1, NW):
        z_arrival(S2, Z2, zs2, zr2, k).wait_recv()
    for k in FAR_G:
        g_copy(Z2, G2, gs2, gr2, k, 4).start()
    G2[:, pl.ds(g, 1), :] = Z2[:, pl.ds(g // 4, 1), :]
    for k in range(1, NG):
        g_arrival(Z2, G2, gs2, gr2, k, 4).wait_recv()

    bands = G2[...].reshape(NPOS, 128)
    quarter = lax.rem(g, 4)
    bands = jnp.where(quarter == 1, pltpu.roll(bands, 96, 1), bands)
    bands = jnp.where(quarter == 2, pltpu.roll(bands, 64, 1), bands)
    bands = jnp.where(quarter == 3, pltpu.roll(bands, 32, 1), bands)
    for r in range(4):
        WT[pl.ds(r, NPOS, stride=4), :] = pltpu.roll(bands, 128 - 8 * r, 1) if r else bands
    weighted = (WT[...].T[:8, :] * quad[...]).astype(BF16)
    found = lax.dot_general(weighted, LV[...], NT, preferred_element_type=F32)
    found = jnp.where(degree < NDEG - own_wave, found, 0.0)
    for p in range(2):
        for k in range(3):
            sout[p, k, 0] = found[3 * p + k : 3 * p + k + 1, :]

    result.wait()
    for k in range(1, NW):
        z_copy(S, Z1, zs, zr, k).wait_send()
        z_copy(S2, Z2, zs2, zr2, k).wait_send()
    for k in range(1, NG):
        g_copy(Z1, G1, gs, gr, k, 2).wait_send()
        g_copy(Z2, G2, gs2, gr2, k, 4).wait_send()
    for k in range(NL):
        if k:
            l_copy(k).wait_send()
            p_copy(k).wait_send()
        for side in range(2):
            e_copy(side, k).wait_send()
    for side in range(2):
        h_copy(side).wait_send()


def body(spectra, legendre, wavenumbers, quad_weights, tracers, kinetics, photolysis, heat_weights):
    vmem = pl.BlockSpec(memory_space=pltpu.VMEM)
    smem = pl.BlockSpec(memory_space=pltpu.SMEM)
    hbm = pl.BlockSpec(memory_space=pl.ANY)
    V, DMA = pltpu.VMEM, pltpu.SemaphoreType.DMA
    return pl.pallas_call(
        kernel,
        out_shape=(
            jax.ShapeDtypeStruct((8, 1, 4, NLON), F32),
            jax.ShapeDtypeStruct((2, 3, 1, 1, NDEG), F32),
        ),
        in_specs=[vmem, hbm, smem, vmem, hbm, smem, smem, smem],
        out_specs=(hbm, vmem),
        scratch_shapes=[
            V((8, 8, NLON), F32), V((8, 8, NLON), F32), V((8, 8, NLON), F32),
            V((NDEG, NLAT), BF16), V((8, NDEG), F32),
            V((NLAT, 128), F32), V((NW, 4, 128), F32), V((NW, 4, 128), F32), V((NW, NG, 128), F32),
            V((128, 128), F32),
            V((NL, 4, CHUNK), F32), V((NL, 4, CHUNK), F32), V((8, NLON), F32),
            V((7, 8, NLON), F32),
            V((2, 16, 128), F32), V((256, 256), BF16), V((256, 256), BF16),
            V((32, 24, 128), F32), V((64, 128), F32),
            V((NW, 2, 128), F32), V((NW, 2, 128), F32), V((NW, NG, 128), F32),
            V((NLAT, 128), F32), V((128, 128), jnp.int32),
            DMA((6,)), DMA((NW,)), DMA((NW,)), DMA((NG,)), DMA((NG,)), DMA((NL,)), DMA((NL,)),
            DMA((NL,)), DMA((NL,)), DMA((2, NL)), DMA((2, NL)), DMA((2,)), DMA((2,)),
            DMA((NW,)), DMA((NW,)), DMA((NG,)), DMA((NG,)),
        ],
        compiler_params=pltpu.CompilerParams(collective_id=0, has_side_effects=True),
    )(
        spectra, legendre, wavenumbers, quad_weights.reshape(1, NLAT), tracers,
        kinetics, photolysis, heat_weights,
    )


def solution(mesh):
    return jax.shard_map(
        body,
        mesh=mesh,
        in_specs=(
            P(None, None, "lev", ("wave", "grp"), None),
            P(("wave", "grp"), None, None),
            P(),
            P(),
            P(None, "lev", ("wave", "grp"), None),
            P(),
            P(),
            P(),
        ),
        out_specs=(
            P(None, "lev", ("wave", "grp"), None),
            P(None, None, "lev", ("wave", "grp"), None),
        ),
        check_vma=False,
    )
```

time: 123 us -> 56.1 us (0.46)
  starting transfers between devices: 51.3 us -> 0 us
  Pallas kernels: 0 us -> 50.1 us
  waiting for transfers between devices: 34.2 us -> 0 us
  other arithmetic: 11.7 us -> 0 us
  matrix products: 10.4 us -> 0 us
  local copies, waits for them, and re-layouts: 12.9 us -> 5.09 us
    pallas_call x0 -> x1, Pallas kernels: none -> 50.1 us  [body(): pl.pallas_call(kernel, out_shape=(jax.ShapeDtypeStruct((8, 1, 4, NLON), F...]
    all_to_all x3 -> x0, starting transfers between devices: 39.1 us -> none  [the longest x1 20 us: body(): lax.all_to_all(fourier, ('wave', 'grp'), split_axis=3, concat_axis=2, til...]
    all_to_all x3 -> x0, waiting for transfers between devices: 30.1 us -> none  [the longest x1 17.7 us: body(): lax.all_to_all(heat_fourier, ('wave', 'grp'), split_axis=2, concat_axis=3...]
    ppermute x4 -> x0, starting transfers between devices: 12.2 us -> none  [the longest x2 8.18 us: with_halo(): lax.ppermute(last, axis, up)]
    dot_general x7 -> x0, matrix products: 10.4 us -> none  [the longest x1 3.64 us: body(): jnp.einsum('pksy,psx->kyx', lax.all_to_all(fourier, ('wave', 'grp'), spli...]
    cos x1 -> x0, other arithmetic: 7.45 us -> none  [fourier_table(): return jnp.stack([jnp.cos(angles), -jnp.sin(angles)])]
    ppermute x4 -> x0, waiting for transfers between devices: 4.11 us -> none  [the longest x2 4.1 us: with_halo(): lax.ppermute(first, axis, [(b, a) for a, b in up])]
    slice x8 -> x0, local copies, waits for them, and re-layouts: 2.82 us -> none  [the longest x4 2.06 us: advect(): eastern = jnp.roll(centre, -1, axis=-1)]
  transfers between devices with their start and end apart: 7 -> 0, of which waited for: 4 -> 0; matrix products, arithmetic and copies ran while one was open for 18% -> 0% of each run, Pallas kernels for 0% -> 0%
where the time goes in v1:
time: 56.1 us; the launch traced here: 55.8 us
  Pallas kernels  50.1 us (89%)
  local copies, waits for them, and re-layouts  5.09 us (9%)
  between operations  0.65 us (1%)
    pallas_call x1, Pallas kernels, body(): pl.pallas_call(kernel, out_shape=(jax.ShapeDtypeStruct((8, 1, 4, NLON), F...  50.1 us
    unnamed x5, local copies, waits for them, and re-layouts  3.85 us
    reshape x1, local copies, waits for them, and re-layouts, body(): quad_weights.reshape(1, NLAT)  1.25 us

profile of v1, /device:TPU:1, one launch (start us, length us, event | category | flops | bytes accessed | tf_op | source)
XLA Modules:
  0.0 55.8 jit_solution(16306292253549063502)
XLA Ops:
  0.6 1.2 %reshape.7.quad = f32[1,384]{1,0:T(1,128)} reshape(f32[384]{0:T(512)} %param.11) | data formatting | bytes 3072 | tf_op jit(solution)/shard_map/reshape | solution.py:420
  1.9 1.4 %copy.10.spec = bf16[2,4,1,1,1024]{4,3,2,1,0:T(2,128)(2,1)} copy(bf16[2,4,1,1,1024]{4,1,3,2,0:T(4,128)(2,1)} %param.8) | data formatting | bytes 32768 | tf_op args[0]
  3.2 50.1 %shard_map.95 = (f32[8,1,4,4096]{3,2,1,0:T(4,128)}, f32[2,3,1,1,1024]{4,3,2,1,0:T(1,128)}) custom-call(bf16[2,4,1,1,1024]{4,3,2,1,0:T(2,128)(2,1)} %copy.10.spec, bf16[1,1024,384]{2,1,0:T(8,128)(2,1)} %leg.1, s32[96]{0:T(128)} %wn.1, f32[1,384]{1,0:T(1,128)} %reshape.7.quad, f32[8,1,4,4096]{3,2,1,0:T(4,128)} %trc.1, f32[8,8]{1,0:T(8,128)} %kin.1, f32[8]{0:T(128)} %pho.1, ...), custom_call_target="tpu_custom_call" | custom-call | tf_op jit(solution)/shard_map/pallas_call | solution.py:395
  53.3 0.0 copy-start
  53.3 1.9 %copy.13 = f32[8,1,4,4096]{3,2,1,0:T(4,128)} copy(f32[8,1,4,4096]{3,2,1,0:T(4,128)} %get-tuple-element.4) | data formatting | bytes 1048576
  55.2 0.0 copy-done
  55.2 0.6 %copy.14 = f32[2,3,1,1,1024]{4,3,2,1,0:T(1,128)} copy(f32[2,3,1,1,1024]{4,3,2,1,0:T(1,128)S(1)} %copy-done) | data formatting | bytes 49152
Async XLA Ops:
  53.3 1.9 %copy-start = (f32[2,3,1,1,1024]{4,3,2,1,0:T(1,128)S(1)}, f32[2,3,1,1,1024]{4,3,2,1,0:T(1,128)}, u32[]{:S(2)}) copy-start(f32[2,3,1,1,1024]{4,3,2,1,0:T(1,128)} %get-tuple-element.5) | copy-start | bytes 73732

commit v2 on v1

--- a/solution.py
+++ b/solution.py
@@ -50,9 +50,9 @@
 
 
 def kernel(
-    spec, leg, wn, quad, trc, kin, pho, hw,
+    spec_in, leg, wn_in, quad_in, trc, kin_in, pho_in, hw_in,
     tout, sout,
-    C, D, O, LV, X, T, S, Z1, G1, V, LR, PC, PH, COEF, AT, BH, BL, H, HF, S2, Z2, G2, WT, WC,
+    spec, wn, quad, kin, pho, hw, C, D, O, M, Q, HN, KP, LV, X, T, S, Z1, G1, V, LR, PC, PH, COEF, AT, BH, BL, H, HF, S2, Z2, G2, WT, WC,
     local, zs, zr, gs, gr, ls, lr, ps, pr, es, er, hs, hr, zs2, zr2, gs2, gr2,
 ):
     w = lax.axis_index("wave")
@@ -63,13 +63,6 @@
     down = lax.rem(pos + NPOS - 1, NPOS)
     up_w, up_g = up // NG, lax.rem(up, NG)
     down_w, down_g = down // NG, lax.rem(down, NG)
-
-    for i in range(4):
-        rows = pl.ds(256 * i, 256)
-        pltpu.make_async_copy(leg.at[0, rows, :], LV.at[rows, :], local.at[i]).start()
-    own_rows = pltpu.make_async_copy(trc.at[:, 0], C.at[:, pl.ds(2, 4), :], local.at[4])
-    own_rows.start()
-    PH[...] = jnp.zeros_like(PH)
 
     barrier = pltpu.get_barrier_semaphore()
 
@@ -88,10 +81,28 @@
         hello(w, l, lax.rem(g + k, NG))
     count = (NW - 1) + (NG - 1) + (NL - 1) + 2 * NL
 
+    for i in range(4):
+        rows = pl.ds(256 * i, 256)
+        pltpu.make_async_copy(leg.at[0, rows, :], LV.at[rows, :], local.at[i]).start()
+    own_rows = pltpu.make_async_copy(trc.at[:, 0], C.at[:, pl.ds(2, 4), :], local.at[4])
+    own_rows.start()
+    small = [
+        pltpu.make_async_copy(src, dst, local.at[6 + i])
+        for i, (src, dst) in enumerate(
+            ((spec_in, spec), (wn_in, wn), (quad_in, quad), (kin_in, kin), (pho_in, pho), (hw_in, hw))
+        )
+    ]
+    for copy in small:
+        copy.start()
+    for row in (0, 7):
+        PH[pl.ds(row, 1), :] = jnp.zeros((1, NLON), F32)
+
+    small[0].wait()
+    small[1].wait()
     own_wave = wn[pos]
     for p in range(2):
         for f in range(4):
-            X[pl.ds(4 * p + f, 1), :] = spec[p, f, 0].astype(F32)
+            X[pl.ds(4 * p + f, 1), :] = spec[p, 0, 0, pl.ds(f, 1), :].astype(F32)
     degree = lax.broadcasted_iota(jnp.int32, (8, NDEG), 1)
     coeffs = jnp.where(degree < NDEG - own_wave, X[...], 0.0).astype(BF16)
     fourier = jnp.zeros((8, NLAT), F32)
@@ -274,52 +285,99 @@
             COEF[5, :, cols] = 0.2 * jnp.exp(0.3 * field[2])
             COEF[6, :, cols] = 1.0 + 0.5 * jnp.tanh(field[3])
 
+    for copy in small[2:]:
+        copy.wait()
+    lane = lax.broadcasted_iota(jnp.int32, (8, 128), 1)
+
+    def transported(here, pick):
+        b = here // 128
+        west = pl.ds(pl.multiple_of(lax.rem(b + 31, 32) * 128, 128), 128)
+        east = pl.ds(pl.multiple_of(lax.rem(b + 1, 32) * 128, 128), 128)
+        here = pl.ds(pl.multiple_of(here, 128), 128)
+        cc, xp, xm, yp, ym = [COEF[i, :, here] for i in range(5)]
+
+        def of(t):
+            c = pick(t, here)
+            western = pltpu.roll(jnp.where(lane == 127, pick(t, west), c), 1, 1)
+            eastern = pltpu.roll(jnp.where(lane == 0, pick(t, east), c), 127, 1)
+            northern = pltpu.roll(c, 1, 0)
+            southern = pltpu.roll(c, 7, 0)
+            return cc * c + xp * western + xm * eastern + yp * northern + ym * southern
+
+        return of
+
+    def transport(src, dst):
+        def block(b, carry):
+            of = transported(b * 128, lambda t, cols: src[t, :, cols])
+            for t in range(8):
+                dst[t, :, pl.ds(pl.multiple_of(b * 128, 128), 128)] = of(t)
+            return carry
+
+        lax.fori_loop(0, 32, block, 0, unroll=2)
+
+    def mix(src, dst, heats):
+        def block(b, carry):
+            cols = pl.ds(pl.multiple_of(b * 512, 512), 512)
+            rate = COEF[5, :, cols]
+            moved = [src[t, :, cols] for t in range(8)]
+            heat = [None] * 3
+            for i in range(8):
+                mixed = kin[i, 0] * moved[0]
+                for t in range(1, 8):
+                    mixed += kin[i, t] * moved[t]
+                done = moved[i] + rate * mixed
+                dst[i, :, cols] = done
+                if heats:
+                    heat = [
+                        hw[k, i] * done if old is None else old + hw[k, i] * done
+                        for k, old in enumerate(heat)
+                    ]
+            if heats:
+                for k in range(3):
+                    HN[k, :, cols] = heat[k]
+            return carry
+
+        lax.fori_loop(0, 8, block, 0)
+
+    transport(C, M)
+    mix(M, D, False)
+    transport(D, O)
+    mix(O, D, True)
+    for i in range(8):
+        total = jnp.full((8, 128), kin[i, 0] * pho[0], F32)
+        for t in range(1, 8):
+            total += jnp.full((8, 128), kin[i, t] * pho[t], F32)
+        KP[i] = total
+    for k in range(3):
+        first = jnp.full((8, 128), hw[k, 0] * pho[0], F32)
+        second = hw[k, 0] * KP[0]
+        for t in range(1, 8):
+            first += jnp.full((8, 128), hw[k, t] * pho[t], F32)
+            second += hw[k, t] * KP[t]
+        KP[8 + k] = first
+        KP[11 + k] = second
+
     for k in range(NL):
         if k:
             p_copy(k, True).wait_recv()
         for side in range(2):
             e_copy(side, k, True).wait_recv()
-
-    lane = lax.broadcasted_iota(jnp.int32, (8, 128), 1)
-
-    def substep(src, dst, last):
-        def block(b, carry):
-            here = pl.ds(pl.multiple_of(b * 128, 128), 128)
-            west = pl.ds(pl.multiple_of(lax.rem(b + 31, 32) * 128, 128), 128)
-            east = pl.ds(pl.multiple_of(lax.rem(b + 1, 32) * 128, 128), 128)
-            cc, xp, xm, yp, ym = [COEF[i, :, here] for i in range(5)]
-            moved = []
-            for t in range(8):
-                c = src[t, :, here]
-                western = pltpu.roll(jnp.where(lane == 127, src[t, :, west], c), 1, 1)
-                eastern = pltpu.roll(jnp.where(lane == 0, src[t, :, east], c), 127, 1)
-                northern = pltpu.roll(c, 1, 0)
-                southern = pltpu.roll(c, 7, 0)
-                moved.append(cc * c + xp * western + xm * eastern + yp * northern + ym * southern)
-            rate = COEF[5, :, here]
-            light = PH[:, here] * moved[0]
-            done = []
-            for i in range(8):
-                mixed = kin[i, 0] * moved[0]
-                for t in range(1, 8):
-                    mixed += kin[i, t] * moved[t]
-                done.append(moved[i] + rate * mixed + pho[i] * light)
-                dst[i, :, here] = done[i]
-            if last:
-                gain = COEF[6, :, here]
-                for k in range(3):
-                    heat = hw[k, 0] * done[0]
-                    for t in range(1, 8):
-                        heat += hw[k, t] * done[t]
-                    H[b, pl.ds(8 * k, 8), :] = heat * gain
-            return carry
-
-        lax.fori_loop(0, 32, block, 0, unroll=2)
-
-    substep(C, D, False)
-    substep(D, O, True)
-    result = pltpu.make_async_copy(O.at[:, pl.ds(2, 4), :], tout.at[:, 0], local.at[5])
-    result.start()
+    Q[...] = PH[...] * M[0]
+
+    def finish(b, carry):
+        here = pl.ds(pl.multiple_of(b * 128, 128), 128)
+        lit = transported(b * 128, lambda t, cols: Q[:, cols])(0)
+        both = lit + PH[:, here] * (O[0, :, here] + pho[0] * lit)
+        late = COEF[5, :, here] * lit
+        for i in range(8):
+            done = D[i, :, here] + (pho[i] * both + KP[i] * late)
+            tout[i, 0, :, here] = done[2:6, :]
+        gain = COEF[6, :, here]
+        for k in range(3):
+            H[b, pl.ds(8 * k, 8), :] = (HN[k, :, here] + (KP[8 + k] * both + KP[11 + k] * late)) * gain
+        return carry
+
+    lax.fori_loop(0, 32, finish, 0, unroll=2)
 
     zr_sum = jnp.zeros((24, 128), F32)
     zi_sum = jnp.zeros((24, 128), F32)
@@ -363,14 +421,13 @@
     bands = jnp.where(quarter == 3, pltpu.roll(bands, 32, 1), bands)
     for r in range(4):
         WT[pl.ds(r, NPOS, stride=4), :] = pltpu.roll(bands, 128 - 8 * r, 1) if r else bands
-    weighted = (WT[...].T[:8, :] * quad[...]).astype(BF16)
+    weighted = (WT[...].T[:8, :] * quad[...].reshape(1, NLAT)).astype(BF16)
     found = lax.dot_general(weighted, LV[...], NT, preferred_element_type=F32)
     found = jnp.where(degree < NDEG - own_wave, found, 0.0)
     for p in range(2):
         for k in range(3):
             sout[p, k, 0] = found[3 * p + k : 3 * p + k + 1, :]
 
-    result.wait()
     for k in range(1, NW):
         z_copy(S, Z1, zs, zr, k).wait_send()
         z_copy(S2, Z2, zs2, zr2, k).wait_send()
@@ -389,19 +446,21 @@
 
 def body(spectra, legendre, wavenumbers, quad_weights, tracers, kinetics, photolysis, heat_weights):
     vmem = pl.BlockSpec(memory_space=pltpu.VMEM)
-    smem = pl.BlockSpec(memory_space=pltpu.SMEM)
     hbm = pl.BlockSpec(memory_space=pl.ANY)
     V, DMA = pltpu.VMEM, pltpu.SemaphoreType.DMA
     return pl.pallas_call(
         kernel,
         out_shape=(
-            jax.ShapeDtypeStruct((8, 1, 4, NLON), F32),
-            jax.ShapeDtypeStruct((2, 3, 1, 1, NDEG), F32),
+            V((8, 1, 4, NLON), F32),
+            V((2, 3, 1, 1, NDEG), F32),
         ),
-        in_specs=[vmem, hbm, smem, vmem, hbm, smem, smem, smem],
-        out_specs=(hbm, vmem),
+        in_specs=[hbm] * 8,
+        out_specs=(vmem, vmem),
         scratch_shapes=[
-            V((8, 8, NLON), F32), V((8, 8, NLON), F32), V((8, 8, NLON), F32),
+            V((2, 1, 1, 4, NDEG), BF16), pltpu.SMEM((NPOS,), jnp.int32), V((NLAT,), F32),
+            pltpu.SMEM((8, 8), F32), pltpu.SMEM((8,), F32), pltpu.SMEM((3, 8), F32),
+            V((8, 8, NLON), F32), V((8, 8, NLON), F32), V((8, 8, NLON), F32), V((8, 8, NLON), F32),
+            V((8, NLON), F32), V((3, 8, NLON), F32), V((14, 8, 128), F32),
             V((NDEG, NLAT), BF16), V((8, NDEG), F32),
             V((NLAT, 128), F32), V((NW, 4, 128), F32), V((NW, 4, 128), F32), V((NW, NG, 128), F32),
             V((128, 128), F32),
@@ -411,14 +470,14 @@
             V((32, 24, 128), F32), V((64, 128), F32),
             V((NW, 2, 128), F32), V((NW, 2, 128), F32), V((NW, NG, 128), F32),
             V((NLAT, 128), F32), V((128, 128), jnp.int32),
-            DMA((6,)), DMA((NW,)), DMA((NW,)), DMA((NG,)), DMA((NG,)), DMA((NL,)), DMA((NL,)),
+            DMA((12,)), DMA((NW,)), DMA((NW,)), DMA((NG,)), DMA((NG,)), DMA((NL,)), DMA((NL,)),
             DMA((NL,)), DMA((NL,)), DMA((2, NL)), DMA((2, NL)), DMA((2,)), DMA((2,)),
             DMA((NW,)), DMA((NW,)), DMA((NG,)), DMA((NG,)),
         ],
         compiler_params=pltpu.CompilerParams(collective_id=0, has_side_effects=True),
     )(
-        spectra, legendre, wavenumbers, quad_weights.reshape(1, NLAT), tracers,
-        kinetics, photolysis, heat_weights,
+        spectra.transpose(0, 2, 3, 1, 4), legendre, wavenumbers, quad_weights, tracers, kinetics,
+        photolysis, heat_weights,
     )
 
 

time: 56.1 us -> 52.9 us (0.943)
  local copies, waits for them, and re-layouts: 5.09 us -> 1.4 us
  Pallas kernels: 50.1 us -> 50.7 us
    unnamed x5 -> x2, local copies, waits for them, and re-layouts: 3.85 us -> 1.4 us
    reshape x1 -> x0, local copies, waits for them, and re-layouts: 1.25 us -> none  [body(): quad_weights.reshape(1, NLAT)]
    pallas_call x1, Pallas kernels: 50.1 us -> 50.7 us  [body(): pl.pallas_call(kernel, out_shape=(V((8, 1, 4, NLON), F32), V((2, 3, 1, 1,...]
where the time goes in v2:
time: 52.9 us; the launch traced here: 52.7 us
  Pallas kernels  50.7 us (96%)
  local copies, waits for them, and re-layouts  1.4 us (3%)
  between operations  0.64 us (1%)
    pallas_call x1, Pallas kernels, body(): pl.pallas_call(kernel, out_shape=(V((8, 1, 4, NLON), F32), V((2, 3, 1, 1,...  50.7 us
    unnamed x2, local copies, waits for them, and re-layouts  1.4 us

profile of v2, /device:TPU:1, one launch (start us, length us, event | category | flops | bytes accessed | tf_op | source)
XLA Modules:
  0.0 52.7 jit_solution(11249796858702765506)
XLA Ops:
  0.6 50.7 %shard_map.95 = (f32[8,1,4,4096]{3,2,1,0:T(4,128)S(1)}, f32[2,3,1,1,1024]{4,3,2,1,0:T(1,128)S(1)}) custom-call(bf16[2,1,1,4,1024]{4,3,2,1,0:T(4,128)(2,1)} %bitcast.1, bf16[1,1024,384]{2,1,0:T(8,128)(2,1)} %leg.1, s32[96]{0:T(128)} %wn_in.1, f32[384]{0:T(512)} %quad_in.1, f32[8,1,4,4096]{3,2,1,0:T(4,128)} %trc.1, f32[8,8]{1,0:T(8,128)} %kin_in.1, f32[8]{0:T(128)} %pho_in.1, ...), custom_call_target="tpu_custom_call" | custom-call | tf_op jit(solution)/shard_map/pallas_call | solution.py:451
  51.3 0.8 %copy.12 = f32[8,1,4,4096]{3,2,1,0:T(4,128)} copy(f32[8,1,4,4096]{3,2,1,0:T(4,128)S(1)} %get-tuple-element.2) | data formatting | bytes 1048576
  52.1 0.6 %copy.13 = f32[2,3,1,1,1024]{4,3,2,1,0:T(1,128)} copy(f32[2,3,1,1,1024]{4,3,2,1,0:T(1,128)S(1)} %get-tuple-element.3) | data formatting | bytes 49152

commit v3 on v2

--- a/solution.py
+++ b/solution.py
@@ -22,6 +22,15 @@
 FAR_L = (4, 3, 5, 2, 6, 1, 7)
 
 
+def hops(peer):
+    dw, dx = peer[0], peer[1] // 2
+    return min(dw, NW - dw) + min(dx, NG // 2 - dx)
+
+
+PEERS = sorted(((dw, dg) for dw in range(NW) for dg in range(NG) if dw or dg), key=hops, reverse=True)
+LANES = pl.ds(0, 128)
+
+
 def cos_sin(m):
     shifted = m + NLON // 8
     quarter = (shifted >> 10) & 3
@@ -52,8 +61,8 @@
 def kernel(
     spec_in, leg, wn_in, quad_in, trc, kin_in, pho_in, hw_in,
     tout, sout,
-    spec, wn, quad, kin, pho, hw, C, D, O, M, Q, HN, KP, LV, X, T, S, Z1, G1, V, LR, PC, PH, COEF, AT, BH, BL, H, HF, S2, Z2, G2, WT, WC,
-    local, zs, zr, gs, gr, ls, lr, ps, pr, es, er, hs, hr, zs2, zr2, gs2, gr2,
+    spec, wn, quad, kin, pho, hw, C, D, O, M, Q, HN, KP, LV, X, T, S, Z1, G1, V, LR, PC, PH, COEF, AT, BH, BL, H, HF, S2, G2, WT, WC,
+    local, zs, zr, gs, gr, ls, lr, ps, pr, es, er, hs, hr, zs2, zr2,
 ):
     w = lax.axis_index("wave")
     l = lax.axis_index("lev")
@@ -63,6 +72,20 @@
     down = lax.rem(pos + NPOS - 1, NPOS)
     up_w, up_g = up // NG, lax.rem(up, NG)
     down_w, down_g = down // NG, lax.rem(down, NG)
+
+    for i in range(4):
+        rows = pl.ds(256 * i, 256)
+        pltpu.make_async_copy(leg.at[0, rows, :], LV.at[rows, :], local.at[i]).start()
+    own_rows = pltpu.make_async_copy(trc.at[:, 0], C.at[:, pl.ds(2, 4), :], local.at[4])
+    own_rows.start()
+    small = [
+        pltpu.make_async_copy(src, dst, local.at[6 + i])
+        for i, (src, dst) in enumerate(
+            ((spec_in, spec), (wn_in, wn), (quad_in, quad), (kin_in, kin), (pho_in, pho), (hw_in, hw))
+        )
+    ]
+    for copy in small:
+        copy.start()
 
     barrier = pltpu.get_barrier_semaphore()
 
@@ -81,19 +104,6 @@
         hello(w, l, lax.rem(g + k, NG))
     count = (NW - 1) + (NG - 1) + (NL - 1) + 2 * NL
 
-    for i in range(4):
-        rows = pl.ds(256 * i, 256)
-        pltpu.make_async_copy(leg.at[0, rows, :], LV.at[rows, :], local.at[i]).start()
-    own_rows = pltpu.make_async_copy(trc.at[:, 0], C.at[:, pl.ds(2, 4), :], local.at[4])
-    own_rows.start()
-    small = [
-        pltpu.make_async_copy(src, dst, local.at[6 + i])
-        for i, (src, dst) in enumerate(
-            ((spec_in, spec), (wn_in, wn), (quad_in, quad), (kin_in, kin), (pho_in, pho), (hw_in, hw))
-        )
-    ]
-    for copy in small:
-        copy.start()
     for row in (0, 7):
         PH[pl.ds(row, 1), :] = jnp.zeros((1, NLON), F32)
 
@@ -313,7 +323,7 @@
                 dst[t, :, pl.ds(pl.multiple_of(b * 128, 128), 128)] = of(t)
             return carry
 
-        lax.fori_loop(0, 32, block, 0, unroll=2)
+        lax.fori_loop(0, 32, block, 0, unroll=8)
 
     def mix(src, dst, heats):
         def block(b, carry):
@@ -377,7 +387,7 @@
             H[b, pl.ds(8 * k, 8), :] = (HN[k, :, here] + (KP[8 + k] * both + KP[11 + k] * late)) * gain
         return carry
 
-    lax.fori_loop(0, 32, finish, 0, unroll=2)
+    lax.fori_loop(0, 32, finish, 0, unroll=4)
 
     zr_sum = jnp.zeros((24, 128), F32)
     zi_sum = jnp.zeros((24, 128), F32)
@@ -399,26 +409,26 @@
     HF[pl.ds(24, 24), :] = zi_sum * scale
     HF[pl.ds(48, 16), :] = jnp.zeros((16, 128), F32)
     mine = jnp.concatenate([HF[pl.ds(r, 8, stride=8), :] for r in range(2, 6)], axis=0)
-    V[...] = jnp.concatenate(
-        [pltpu.roll(mine, 128 - d, 1) if d else mine for d in range(4)], axis=0
-    ).T
-    S2[...] = V[pl.ds(0, 24, stride=4), :].reshape(NW, 2, 128)
-    for k in FAR_W:
-        z_copy(S2, Z2, zs2, zr2, k).start()
-    Z2[w] = S2[w]
-    for k in range(1, NW):
-        z_arrival(S2, Z2, zs2, zr2, k).wait_recv()
-    for k in FAR_G:
-        g_copy(Z2, G2, gs2, gr2, k, 4).start()
-    G2[:, pl.ds(g, 1), :] = Z2[:, pl.ds(g // 4, 1), :]
-    for k in range(1, NG):
-        g_arrival(Z2, G2, gs2, gr2, k, 4).wait_recv()
-
-    bands = G2[...].reshape(NPOS, 128)
-    quarter = lax.rem(g, 4)
-    bands = jnp.where(quarter == 1, pltpu.roll(bands, 96, 1), bands)
-    bands = jnp.where(quarter == 2, pltpu.roll(bands, 64, 1), bands)
-    bands = jnp.where(quarter == 3, pltpu.roll(bands, 32, 1), bands)
+    S2[:, pl.ds(0, 32)] = mine.T
+
+    def back(dw, dg):
+        there_w, there_g = lax.rem(w + dw, NW), lax.rem(g + dg, NG)
+        return pltpu.make_async_remote_copy(
+            S2.at[pl.ds(there_w * NG + there_g, 1), LANES], G2.at[pl.ds(pos, 1), LANES],
+            zs2.at[0], zr2.at[0],
+            device_id=(there_w, l, there_g), device_id_type=MESH,
+        )
+
+    for dw, dg in PEERS:
+        back(dw, dg).start()
+    G2[pl.ds(pos, 1), :] = S2[pl.ds(pos, 1), :]
+    every = pltpu.make_async_remote_copy(
+        S2.at[pl.ds(0, NPOS - 1), LANES], G2.at[pl.ds(0, NPOS - 1), LANES], zs2.at[0], zr2.at[0],
+        device_id=(up_w, l, up_g), device_id_type=MESH,
+    )
+    every.wait_recv()
+
+    bands = G2[...]
     for r in range(4):
         WT[pl.ds(r, NPOS, stride=4), :] = pltpu.roll(bands, 128 - 8 * r, 1) if r else bands
     weighted = (WT[...].T[:8, :] * quad[...].reshape(1, NLAT)).astype(BF16)
@@ -428,12 +438,11 @@
         for k in range(3):
             sout[p, k, 0] = found[3 * p + k : 3 * p + k + 1, :]
 
+    every.wait_send()
     for k in range(1, NW):
         z_copy(S, Z1, zs, zr, k).wait_send()
-        z_copy(S2, Z2, zs2, zr2, k).wait_send()
     for k in range(1, NG):
         g_copy(Z1, G1, gs, gr, k, 2).wait_send()
-        g_copy(Z2, G2, gs2, gr2, k, 4).wait_send()
     for k in range(NL):
         if k:
             l_copy(k).wait_send()
@@ -468,11 +477,11 @@
             V((7, 8, NLON), F32),
             V((2, 16, 128), F32), V((256, 256), BF16), V((256, 256), BF16),
             V((32, 24, 128), F32), V((64, 128), F32),
-            V((NW, 2, 128), F32), V((NW, 2, 128), F32), V((NW, NG, 128), F32),
+            V((128, 128), F32), V((NPOS, 128), F32),
             V((NLAT, 128), F32), V((128, 128), jnp.int32),
             DMA((12,)), DMA((NW,)), DMA((NW,)), DMA((NG,)), DMA((NG,)), DMA((NL,)), DMA((NL,)),
             DMA((NL,)), DMA((NL,)), DMA((2, NL)), DMA((2, NL)), DMA((2,)), DMA((2,)),
-            DMA((NW,)), DMA((NW,)), DMA((NG,)), DMA((NG,)),
+            DMA((1,)), DMA((1,)),
         ],
         compiler_params=pltpu.CompilerParams(collective_id=0, has_side_effects=True),
     )(

time: 52.9 us -> 47.2 us (0.89)
  Pallas kernels: 50.7 us -> 45 us
    pallas_call x1, Pallas kernels: 50.7 us -> 45 us  [body(): pl.pallas_call(kernel, out_shape=(V((8, 1, 4, NLON), F32), V((2, 3, 1, 1,...]
where the time goes in v3:
time: 47.2 us; the launch traced here: 47 us
  Pallas kernels  45 us (95%)
  local copies, waits for them, and re-layouts  1.4 us (3%)
  between operations  0.64 us (1%)
    pallas_call x1, Pallas kernels, body(): pl.pallas_call(kernel, out_shape=(V((8, 1, 4, NLON), F32), V((2, 3, 1, 1,...  45 us
    unnamed x2, local copies, waits for them, and re-layouts  1.4 us

profile of v3, /device:TPU:1, one launch (start us, length us, event | category | flops | bytes accessed | tf_op | source)
XLA Modules:
  0.0 47.0 jit_solution(15963481118658201587)
XLA Ops:
  0.6 45.0 %shard_map.95 = (f32[8,1,4,4096]{3,2,1,0:T(4,128)S(1)}, f32[2,3,1,1,1024]{4,3,2,1,0:T(1,128)S(1)}) custom-call(bf16[2,1,1,4,1024]{4,3,2,1,0:T(4,128)(2,1)} %bitcast.1, bf16[1,1024,384]{2,1,0:T(8,128)(2,1)} %leg.1, s32[96]{0:T(128)} %wn_in.1, f32[384]{0:T(512)} %quad_in.1, f32[8,1,4,4096]{3,2,1,0:T(4,128)} %trc.1, f32[8,8]{1,0:T(8,128)} %kin_in.1, f32[8]{0:T(128)} %pho_in.1, ...), custom_call_target="tpu_custom_call" | custom-call | tf_op jit(solution)/shard_map/pallas_call | solution.py:460
  45.6 0.8 %copy.12 = f32[8,1,4,4096]{3,2,1,0:T(4,128)} copy(f32[8,1,4,4096]{3,2,1,0:T(4,128)S(1)} %get-tuple-element.2) | data formatting | bytes 1048576
  46.4 0.6 %copy.13 = f32[2,3,1,1,1024]{4,3,2,1,0:T(1,128)} copy(f32[2,3,1,1,1024]{4,3,2,1,0:T(1,128)S(1)} %get-tuple-element.3) | data formatting | bytes 49152

commit v4 on v3

--- a/solution.py
+++ b/solution.py
@@ -17,18 +17,26 @@
 BF16 = jnp.bfloat16
 MESH = pl.DeviceIdType.MESH
 NT = (((1,), (1,)), ((), ()))
-FAR_W = (6, 5, 7, 4, 8, 3, 9, 2, 10, 1, 11)
-FAR_G = (4, 3, 5, 2, 6, 7, 1)
 FAR_L = (4, 3, 5, 2, 6, 1, 7)
 
 
-def hops(peer):
-    dw, dx = peer[0], peer[1] // 2
-    return min(dw, NW - dw) + min(dx, NG // 2 - dx)
-
-
-PEERS = sorted(((dw, dg) for dw in range(NW) for dg in range(NG) if dw or dg), key=hops, reverse=True)
-LANES = pl.ds(0, 128)
+def wrapped(i, n):
+    return jnp.where(i >= n, i - n, i)
+
+
+def outward(i, n):
+    return n // 2 + ((i + 1) >> 1) * (1 - 2 * (i & 1))
+
+
+def each_peer(w, g, act):
+    def row(i, carry):
+        for j in range(NG):
+            act(wrapped(w + outward(i, NW), NW), wrapped(g + outward(j, NG), NG))
+        return carry
+
+    lax.fori_loop(0, NW - 1, row, 0)
+    for j in range(NG - 1):
+        act(w, wrapped(g + outward(j, NG), NG))
 
 
 def cos_sin(m):
@@ -61,8 +69,8 @@
 def kernel(
     spec_in, leg, wn_in, quad_in, trc, kin_in, pho_in, hw_in,
     tout, sout,
-    spec, wn, quad, kin, pho, hw, C, D, O, M, Q, HN, KP, LV, X, T, S, Z1, G1, V, LR, PC, PH, COEF, AT, BH, BL, H, HF, S2, G2, WT, WC,
-    local, zs, zr, gs, gr, ls, lr, ps, pr, es, er, hs, hr, zs2, zr2,
+    spec, wn, quad, kin, pho, hw, C, D, O, M, Q, HN, KP, LV, X, T, G1, V, LR, PC, PH, COEF, AT, BH, BL, H, HF, S2, G2, WT, WC,
+    local, gs, gr, ls, lr, ps, pr, es, er, hs, hr, gs2, gr2,
 ):
     w = lax.axis_index("wave")
     l = lax.axis_index("lev")
@@ -92,17 +100,13 @@
     def hello(dw, dl, dg):
         pl.semaphore_signal(barrier, inc=1, device_id=(dw, dl, dg), device_id_type=MESH)
 
-    for k in FAR_W:
-        hello(lax.rem(w + k, NW), l, g)
-    for k in range(NL):
-        ll = lax.rem(l + k, NL)
+    each_peer(w, g, lambda dw, dg: hello(dw, l, dg))
+    for k in FAR_L:
+        ll = wrapped(l + k, NL)
         hello(up_w, ll, up_g)
         hello(down_w, ll, down_g)
-        if k:
-            hello(w, ll, g)
-    for k in FAR_G:
-        hello(w, l, lax.rem(g + k, NG))
-    count = (NW - 1) + (NG - 1) + (NL - 1) + 2 * NL
+        hello(w, ll, g)
+    count = NPOS - 1 + 3 * (NL - 1)
 
     for row in (0, 7):
         PH[pl.ds(row, 1), :] = jnp.zeros((1, NLON), F32)
@@ -123,42 +127,30 @@
             coeffs[:, 256 * i : 256 * i + 256], LV[rows, :], preferred_element_type=F32
         )
     groups = []
-    for c in range(2):
-        for r in range(8):
-            shift = (NLAT - (4 * c + r - 2)) % NLAT
-            groups.append(pltpu.roll(fourier, shift, 1) if shift else fourier)
-    T[...] = jnp.concatenate(groups, axis=0).T
-    S[...] = T[pl.ds(0, 48, stride=8), :].reshape(NW, 4, 128)
+    for r in range(8):
+        shift = (NLAT + 2 - r) % NLAT
+        groups.append(pltpu.roll(fourier, shift, 1) if shift else fourier)
+    T[:, pl.ds(0, 64)] = jnp.concatenate(groups, axis=0).T
     own_rows.wait()
 
     pl.semaphore_wait(barrier, count)
 
-    def z_copy(src, dst, ssem, rsem, k):
-        there = lax.rem(w + k, NW)
+    def send(src, stride, dst, ssem, rsem):
+        def act(there_w, there_g):
+            pltpu.make_async_remote_copy(
+                src.at[pl.ds((there_w * NG + there_g) * stride, 1)], dst.at[pl.ds(pos, 1)],
+                ssem.at[0], rsem.at[0],
+                device_id=(there_w, l, there_g), device_id_type=MESH,
+            ).start()
+
+        each_peer(w, g, act)
+        dst[pl.ds(pos, 1), :] = src[pl.ds(pos * stride, 1), :]
+
+    def every(src, dst, ssem, rsem):
+        rows = pl.ds(0, NPOS - 1)
         return pltpu.make_async_remote_copy(
-            src.at[there], dst.at[w], ssem.at[k], rsem.at[w],
-            device_id=(there, l, g), device_id_type=MESH,
-        )
-
-    def z_arrival(src, dst, ssem, rsem, k):
-        there = lax.rem(w + k, NW)
-        return pltpu.make_async_remote_copy(
-            src.at[there], dst.at[there], ssem.at[k], rsem.at[there],
-            device_id=(there, l, g), device_id_type=MESH,
-        )
-
-    def g_copy(src, dst, ssem, rsem, k, share):
-        there = lax.rem(g + k, NG)
-        return pltpu.make_async_remote_copy(
-            src.at[:, there // share, :], dst.at[:, g, :], ssem.at[k], rsem.at[g],
-            device_id=(w, l, there), device_id_type=MESH,
-        )
-
-    def g_arrival(src, dst, ssem, rsem, k, share):
-        there = lax.rem(g + k, NG)
-        return pltpu.make_async_remote_copy(
-            src.at[:, there // share, :], dst.at[:, there, :], ssem.at[k], rsem.at[there],
-            device_id=(w, l, there), device_id_type=MESH,
+            src.at[rows], dst.at[rows], ssem.at[0], rsem.at[0],
+            device_id=(up_w, l, up_g), device_id_type=MESH,
         )
 
     def l_copy(k, arrival=False):
@@ -199,13 +191,11 @@
             device_id_type=MESH,
         )
 
-    for k in FAR_W:
-        z_copy(S, Z1, zs, zr, k).start()
+    send(T, 4, G1, gs, gr)
     for k in FAR_L:
         l_copy(k).start()
     for side in range(2):
         h_copy(side).start()
-    Z1[w] = S[w]
     LR[l] = C[0, pl.ds(2, 4), pl.ds(pl.multiple_of(CHUNK * l, CHUNK), CHUNK)]
 
     for s in range(NPOS):
@@ -238,12 +228,6 @@
             e_copy(side, k).start()
     PH[pl.ds(2, 4), pl.ds(pl.multiple_of(CHUNK * l, CHUNK), CHUNK)] = PC[l]
 
-    for k in range(1, NW):
-        z_arrival(S, Z1, zs, zr, k).wait_recv()
-    for k in FAR_G:
-        g_copy(Z1, G1, gs, gr, k, 2).start()
-    G1[:, pl.ds(g, 1), :] = Z1[:, pl.ds(g // 2, 1), :]
-
     for side in range(2):
         h_copy(side).wait_recv()
 
@@ -255,19 +239,13 @@
     def _():
         C[:, pl.ds(6, 2), :] = jnp.zeros((8, 2, NLON), F32)
 
-    for k in range(1, NG):
-        g_arrival(Z1, G1, gs, gr, k, 2).wait_recv()
-
-    arrived = jnp.concatenate([G1[...].reshape(NPOS, 128), jnp.zeros((128 - NPOS, 128), F32)], axis=0)
+    every(T, G1, gs, gr).wait_recv()
+
+    arrived = jnp.concatenate([G1[...], jnp.zeros((128 - NPOS, 128), F32)], axis=0)
     V[...] = arrived.T
-    second = lax.rem(g, 2) == 1
     parts = []
     for p in range(2):
-        fields = []
-        for f in range(4):
-            first = V[pl.ds(4 * p + f, 8, stride=8), :]
-            other = V[pl.ds(64 + 4 * p + f, 8, stride=8), :]
-            fields.append(jnp.where(second, other, first))
+        fields = [V[pl.ds(4 * p + f, 8, stride=8), :] for f in range(4)]
         parts.append(jnp.concatenate(fields, axis=0) * (1.0 / math.sqrt(NPOS)))
     real, imag = parts
     latitude = lax.broadcasted_iota(jnp.int32, (8, 256), 0) + (4 * pos - 2)
@@ -299,11 +277,10 @@
         copy.wait()
     lane = lax.broadcasted_iota(jnp.int32, (8, 128), 1)
 
-    def transported(here, pick):
-        b = here // 128
-        west = pl.ds(pl.multiple_of(lax.rem(b + 31, 32) * 128, 128), 128)
-        east = pl.ds(pl.multiple_of(lax.rem(b + 1, 32) * 128, 128), 128)
-        here = pl.ds(pl.multiple_of(here, 128), 128)
+    def transported(b, pick):
+        west = pl.ds(pl.multiple_of(((b + 31) & 31) * 128, 128), 128)
+        east = pl.ds(pl.multiple_of(((b + 1) & 31) * 128, 128), 128)
+        here = pl.ds(pl.multiple_of(b * 128, 128), 128)
         cc, xp, xm, yp, ym = [COEF[i, :, here] for i in range(5)]
 
         def of(t):
@@ -318,12 +295,12 @@
 
     def transport(src, dst):
         def block(b, carry):
-            of = transported(b * 128, lambda t, cols: src[t, :, cols])
+            of = transported(b, lambda t, cols: src[t, :, cols])
             for t in range(8):
                 dst[t, :, pl.ds(pl.multiple_of(b * 128, 128), 128)] = of(t)
             return carry
 
-        lax.fori_loop(0, 32, block, 0, unroll=8)
+        lax.fori_loop(0, 32, block, 0, unroll=16)
 
     def mix(src, dst, heats):
         def block(b, carry):
@@ -376,7 +353,7 @@
 
     def finish(b, carry):
         here = pl.ds(pl.multiple_of(b * 128, 128), 128)
-        lit = transported(b * 128, lambda t, cols: Q[:, cols])(0)
+        lit = transported(b, lambda t, cols: Q[:, cols])(0)
         both = lit + PH[:, here] * (O[0, :, here] + pho[0] * lit)
         late = COEF[5, :, here] * lit
         for i in range(8):
@@ -411,22 +388,8 @@
     mine = jnp.concatenate([HF[pl.ds(r, 8, stride=8), :] for r in range(2, 6)], axis=0)
     S2[:, pl.ds(0, 32)] = mine.T
 
-    def back(dw, dg):
-        there_w, there_g = lax.rem(w + dw, NW), lax.rem(g + dg, NG)
-        return pltpu.make_async_remote_copy(
-            S2.at[pl.ds(there_w * NG + there_g, 1), LANES], G2.at[pl.ds(pos, 1), LANES],
-            zs2.at[0], zr2.at[0],
-            device_id=(there_w, l, there_g), device_id_type=MESH,
-        )
-
-    for dw, dg in PEERS:
-        back(dw, dg).start()
-    G2[pl.ds(pos, 1), :] = S2[pl.ds(pos, 1), :]
-    every = pltpu.make_async_remote_copy(
-        S2.at[pl.ds(0, NPOS - 1), LANES], G2.at[pl.ds(0, NPOS - 1), LANES], zs2.at[0], zr2.at[0],
-        device_id=(up_w, l, up_g), device_id_type=MESH,
-    )
-    every.wait_recv()
+    send(S2, 1, G2, gs2, gr2)
+    every(S2, G2, gs2, gr2).wait_recv()
 
     bands = G2[...]
     for r in range(4):
@@ -438,11 +401,8 @@
         for k in range(3):
             sout[p, k, 0] = found[3 * p + k : 3 * p + k + 1, :]
 
-    every.wait_send()
-    for k in range(1, NW):
-        z_copy(S, Z1, zs, zr, k).wait_send()
-    for k in range(1, NG):
-        g_copy(Z1, G1, gs, gr, k, 2).wait_send()
+    every(T, G1, gs, gr).wait_send()
+    every(S2, G2, gs2, gr2).wait_send()
     for k in range(NL):
         if k:
             l_copy(k).wait_send()
@@ -453,11 +413,22 @@
         h_copy(side).wait_send()
 
 
+def hand_over(tracers_ref, heating_ref, tracers_out, heating_out, sems):
+    copies = [
+        pltpu.make_async_copy(tracers_ref, tracers_out, sems.at[0]),
+        pltpu.make_async_copy(heating_ref, heating_out, sems.at[1]),
+    ]
+    for copy in copies:
+        copy.start()
+    for copy in copies:
+        copy.wait()
+
+
 def body(spectra, legendre, wavenumbers, quad_weights, tracers, kinetics, photolysis, heat_weights):
     vmem = pl.BlockSpec(memory_space=pltpu.VMEM)
     hbm = pl.BlockSpec(memory_space=pl.ANY)
     V, DMA = pltpu.VMEM, pltpu.SemaphoreType.DMA
-    return pl.pallas_call(
+    tracers_out, heating = pl.pallas_call(
         kernel,
         out_shape=(
             V((8, 1, 4, NLON), F32),
@@ -471,7 +442,7 @@
             V((8, 8, NLON), F32), V((8, 8, NLON), F32), V((8, 8, NLON), F32), V((8, 8, NLON), F32),
             V((8, NLON), F32), V((3, 8, NLON), F32), V((14, 8, 128), F32),
             V((NDEG, NLAT), BF16), V((8, NDEG), F32),
-            V((NLAT, 128), F32), V((NW, 4, 128), F32), V((NW, 4, 128), F32), V((NW, NG, 128), F32),
+            V((NLAT, 128), F32), V((NPOS, 128), F32),
             V((128, 128), F32),
             V((NL, 4, CHUNK), F32), V((NL, 4, CHUNK), F32), V((8, NLON), F32),
             V((7, 8, NLON), F32),
@@ -479,7 +450,7 @@
             V((32, 24, 128), F32), V((64, 128), F32),
             V((128, 128), F32), V((NPOS, 128), F32),
             V((NLAT, 128), F32), V((128, 128), jnp.int32),
-            DMA((12,)), DMA((NW,)), DMA((NW,)), DMA((NG,)), DMA((NG,)), DMA((NL,)), DMA((NL,)),
+            DMA((12,)), DMA((1,)), DMA((1,)), DMA((NL,)), DMA((NL,)),
             DMA((NL,)), DMA((NL,)), DMA((2, NL)), DMA((2, NL)), DMA((2,)), DMA((2,)),
             DMA((1,)), DMA((1,)),
         ],
@@ -487,6 +458,19 @@
     )(
         spectra.transpose(0, 2, 3, 1, 4), legendre, wavenumbers, quad_weights, tracers, kinetics,
         photolysis, heat_weights,
+    )
+    return pl.pallas_call(
+        hand_over,
+        out_shape=(
+            jax.ShapeDtypeStruct((8, 1, 4, NLON), F32),
+            jax.ShapeDtypeStruct((2, 3, 1, 1, NDEG), F32),
+        ),
+        in_specs=[vmem, vmem],
+        out_specs=(hbm, hbm),
+        scratch_shapes=[DMA((2,))],
+    )(
+        pltpu.with_memory_space_constraint(tracers_out, pltpu.VMEM),
+        pltpu.with_memory_space_constraint(heating, pltpu.VMEM),
     )
 
 

time: 47.2 us -> 44.1 us (0.934)
  Pallas kernels: 45 us -> 43.3 us
  local copies, waits for them, and re-layouts: 1.4 us -> 0 us
    pallas_call x1, Pallas kernels: 45 us -> 42.5 us  [body(): pl.pallas_call(kernel, out_shape=(V((8, 1, 4, NLON), F32), V((2, 3, 1, 1,...]
    unnamed x2 -> x0, local copies, waits for them, and re-layouts: 1.4 us -> none
    pallas_call x0 -> x1, Pallas kernels: none -> 0.81 us  [body(): pl.pallas_call(hand_over, out_shape=(jax.ShapeDtypeStruct((8, 1, 4, NLON)...]
where the time goes in v4:
time: 44.1 us; the launch traced here: 43.9 us
  Pallas kernels  43.3 us (98%)
  between operations  0.64 us (1%)
    pallas_call x1, Pallas kernels, body(): pl.pallas_call(kernel, out_shape=(V((8, 1, 4, NLON), F32), V((2, 3, 1, 1,...  42.5 us

profile of v4, /device:TPU:1, one launch (start us, length us, event | category | flops | bytes accessed | tf_op | source)
XLA Modules:
  0.0 43.9 jit_solution(15118603760802439098)
XLA Ops:
  0.6 42.5 %shard_map.95 = (f32[8,1,4,4096]{3,2,1,0:T(4,128)S(1)}, f32[2,3,1,1,1024]{4,3,2,1,0:T(1,128)S(1)}) custom-call(bf16[2,1,1,4,1024]{4,3,2,1,0:T(4,128)(2,1)} %bitcast.1, bf16[1,1024,384]{2,1,0:T(8,128)(2,1)} %leg.1, s32[96]{0:T(128)} %wn_in.1, f32[384]{0:T(512)} %quad_in.1, f32[8,1,4,4096]{3,2,1,0:T(4,128)} %trc.1, f32[8,8]{1,0:T(8,128)} %kin_in.1, f32[8]{0:T(128)} %pho_in.1, ...), custom_call_target="tpu_custom_call" | custom-call | tf_op jit(solution)/shard_map/pallas_call | solution.py:431
  43.1 0.8 %shard_map.96 = (f32[8,1,4,4096]{3,2,1,0:T(4,128)}, f32[2,3,1,1,1024]{4,3,2,1,0:T(1,128)}) custom-call(f32[8,1,4,4096]{3,2,1,0:T(4,128)S(1)} %get-tuple-element.4.tracers_ref, f32[2,3,1,1,1024]{4,3,2,1,0:T(1,128)S(1)} %get-tuple-element.5.heating_ref), custom_call_target="tpu_custom_call" | custom-call | tf_op jit(solution)/shard_map/pallas_call | solution.py:462

commit v5 on v4

--- a/solution.py
+++ b/solution.py
@@ -69,7 +69,7 @@
 def kernel(
     spec_in, leg, wn_in, quad_in, trc, kin_in, pho_in, hw_in,
     tout, sout,
-    spec, wn, quad, kin, pho, hw, C, D, O, M, Q, HN, KP, LV, X, T, G1, V, LR, PC, PH, COEF, AT, BH, BL, H, HF, S2, G2, WT, WC,
+    spec, wn, quad, kin, pho, hw, C, D, O, M, E, Q, HN, KP, CP, AP, LV, X, T, G1, V, LR, PC, PH, COEF, AT, BH, BL, H, HF, S2, G2, WT, WC,
     local, gs, gr, ls, lr, ps, pr, es, er, hs, hr, gs2, gr2,
 ):
     w = lax.axis_index("wave")
@@ -198,6 +198,13 @@
         h_copy(side).start()
     LR[l] = C[0, pl.ds(2, 4), pl.ds(pl.multiple_of(CHUNK * l, CHUNK), CHUNK)]
 
+    upper = lax.broadcasted_iota(jnp.int32, (8, 256), 0) < 4
+
+    def packed(first, second):
+        return jnp.where(
+            upper[:, : first.shape[1]], pltpu.roll(first, 6, 0), pltpu.roll(second, 2, 0)
+        )
+
     for s in range(NPOS):
         WC[pl.ds(s, 1), :] = jnp.full((1, 128), wn[s], jnp.int32)
     WC[pl.ds(NPOS, 128 - NPOS), :] = jnp.zeros((128 - NPOS, 128), jnp.int32)
@@ -205,6 +212,11 @@
     across = waves.astype(F32).T[:16, :].astype(jnp.int32)
     coarse = lax.broadcasted_iota(jnp.int32, (16, 128), 0) * 256
     AT[0], AT[1] = cos_sin((across * coarse) & (NLON - 1))
+    for p in range(2):
+        for j in range(8):
+            low = jnp.broadcast_to(AT[p, pl.ds(j, 1), :], (8, 128))
+            high = jnp.broadcast_to(AT[p, pl.ds(j + 8, 1), :], (8, 128))
+            AP[p, j] = jnp.where(upper[:, :128], low, high)
     used = lax.broadcasted_iota(jnp.int32, (128, 128), 0) < NPOS
     for half in range(2):
         fine = lax.broadcasted_iota(jnp.int32, (128, 128), 1) + 128 * half
@@ -228,6 +240,22 @@
             e_copy(side, k).start()
     PH[pl.ds(2, 4), pl.ds(pl.multiple_of(CHUNK * l, CHUNK), CHUNK)] = PC[l]
 
+    for copy in small[2:]:
+        copy.wait()
+    for i in range(8):
+        total = jnp.full((8, 128), kin[i, 0] * pho[0], F32)
+        for t in range(1, 8):
+            total += jnp.full((8, 128), kin[i, t] * pho[t], F32)
+        KP[i] = total
+    for k in range(3):
+        first = jnp.full((8, 128), hw[k, 0] * pho[0], F32)
+        second = hw[k, 0] * KP[0]
+        for t in range(1, 8):
+            first += jnp.full((8, 128), hw[k, t] * pho[t], F32)
+            second += hw[k, t] * KP[t]
+        KP[8 + k] = first
+        KP[11 + k] = second
+
     for side in range(2):
         h_copy(side).wait_recv()
 
@@ -252,16 +280,17 @@
     inside = jnp.where((latitude >= 0) & (latitude < NLAT), 1.0, 0.0)
     bh, bl = BH[...], BL[...]
     for part in range(4):
+        blocks = (2 * part, 2 * part + 1, 2 * part + 8, 2 * part + 9)
         turned = []
-        for i in range(4):
-            h = 4 * part + i
+        for h in blocks:
             ca, sa = AT[0, pl.ds(h, 1), :], AT[1, pl.ds(h, 1), :]
             turned.append(
                 jnp.concatenate([real * ca - imag * sa, real * sa + imag * ca], axis=1)
             )
         grid = dot3(jnp.concatenate(turned, axis=0), bh, bl, (((1,), (0,)), ((), ())))
-        for i in range(4):
-            cols = pl.ds(256 * (4 * part + i), 256)
+        rates, gains = [], []
+        for i, h in enumerate(blocks):
+            cols = pl.ds(256 * h, 256)
             field = [grid[32 * i + 8 * f : 32 * i + 8 * f + 8, :] for f in range(4)]
             cx = 0.45 * jnp.tanh(field[0]) * inside
             cy = 0.45 * jnp.tanh(field[1]) * inside
@@ -270,11 +299,14 @@
             COEF[2, :, cols] = jnp.maximum(-cx, 0.0)
             COEF[3, :, cols] = jnp.maximum(cy, 0.0)
             COEF[4, :, cols] = jnp.maximum(-cy, 0.0)
-            COEF[5, :, cols] = 0.2 * jnp.exp(0.3 * field[2])
-            COEF[6, :, cols] = 1.0 + 0.5 * jnp.tanh(field[3])
-
-    for copy in small[2:]:
-        copy.wait()
+            rates.append(0.2 * jnp.exp(0.3 * field[2]))
+            COEF[5, :, cols] = rates[i]
+            gains.append(field[3])
+        for i in range(2):
+            cols = pl.ds(256 * blocks[i], 256)
+            CP[0, :, cols] = packed(rates[i], rates[i + 2])
+            CP[1, :, cols] = 1.0 + 0.5 * jnp.tanh(packed(gains[i], gains[i + 2]))
+
     lane = lax.broadcasted_iota(jnp.int32, (8, 128), 1)
 
     def transported(b, pick):
@@ -293,19 +325,23 @@
 
         return of
 
-    def transport(src, dst):
-        def block(b, carry):
-            of = transported(b, lambda t, cols: src[t, :, cols])
-            for t in range(8):
-                dst[t, :, pl.ds(pl.multiple_of(b * 128, 128), 128)] = of(t)
-            return carry
-
-        lax.fori_loop(0, 32, block, 0, unroll=16)
-
-    def mix(src, dst, heats):
+    def transport(b, carry):
+        of = transported(b, lambda t, cols: C[t, :, cols])
+        for t in range(8):
+            M[t, :, pl.ds(pl.multiple_of(b * 128, 128), 128)] = of(t)
+        return carry
+
+    def transport_packed(b, carry):
+        first = transported(b, lambda t, cols: D[t, :, cols])
+        second = transported(b + 16, lambda t, cols: D[t, :, cols])
+        for t in range(8):
+            O[t, :, pl.ds(pl.multiple_of(b * 128, 128), 128)] = packed(first(t), second(t))
+        return carry
+
+    def mix(src, rates, dst, heats):
         def block(b, carry):
             cols = pl.ds(pl.multiple_of(b * 512, 512), 512)
-            rate = COEF[5, :, cols]
+            rate = rates[:, cols]
             moved = [src[t, :, cols] for t in range(8)]
             heat = [None] * 3
             for i in range(8):
@@ -324,26 +360,12 @@
                     HN[k, :, cols] = heat[k]
             return carry
 
-        lax.fori_loop(0, 8, block, 0)
-
-    transport(C, M)
-    mix(M, D, False)
-    transport(D, O)
-    mix(O, D, True)
-    for i in range(8):
-        total = jnp.full((8, 128), kin[i, 0] * pho[0], F32)
-        for t in range(1, 8):
-            total += jnp.full((8, 128), kin[i, t] * pho[t], F32)
-        KP[i] = total
-    for k in range(3):
-        first = jnp.full((8, 128), hw[k, 0] * pho[0], F32)
-        second = hw[k, 0] * KP[0]
-        for t in range(1, 8):
-            first += jnp.full((8, 128), hw[k, t] * pho[t], F32)
-            second += hw[k, t] * KP[t]
-        KP[8 + k] = first
-        KP[11 + k] = second
-
+        lax.fori_loop(0, dst.shape[2] // 512, block, 0)
+
+    lax.fori_loop(0, 32, transport, 0, unroll=16)
+    mix(M, COEF.at[5], D, False)
+    lax.fori_loop(0, 16, transport_packed, 0, unroll=8)
+    mix(O, CP.at[0], E, True)
     for k in range(NL):
         if k:
             p_copy(k, True).wait_recv()
@@ -353,30 +375,36 @@
 
     def finish(b, carry):
         here = pl.ds(pl.multiple_of(b * 128, 128), 128)
-        lit = transported(b, lambda t, cols: Q[:, cols])(0)
-        both = lit + PH[:, here] * (O[0, :, here] + pho[0] * lit)
-        late = COEF[5, :, here] * lit
+        there = pl.ds(pl.multiple_of(b * 128 + 2048, 128), 128)
+        lit = packed(
+            transported(b, lambda t, cols: Q[:, cols])(0),
+            transported(b + 16, lambda t, cols: Q[:, cols])(0),
+        )
+        light = packed(PH[:, here], PH[:, there])
+        both = lit + light * (O[0, :, here] + pho[0] * lit)
+        late = CP[0, :, here] * lit
         for i in range(8):
-            done = D[i, :, here] + (pho[i] * both + KP[i] * late)
-            tout[i, 0, :, here] = done[2:6, :]
-        gain = COEF[6, :, here]
+            done = E[i, :, here] + (pho[i] * both + KP[i] * late)
+            tout[i, 0, :, here] = done[:4, :]
+            tout[i, 0, :, there] = done[4:, :]
+        gain = CP[1, :, here]
         for k in range(3):
             H[b, pl.ds(8 * k, 8), :] = (HN[k, :, here] + (KP[8 + k] * both + KP[11 + k] * late)) * gain
         return carry
 
-    lax.fori_loop(0, 32, finish, 0, unroll=4)
+    lax.fori_loop(0, 16, finish, 0, unroll=4)
 
     zr_sum = jnp.zeros((24, 128), F32)
     zi_sum = jnp.zeros((24, 128), F32)
-    for part in range(4):
+    for part in range(2):
         rows = []
         for i in range(4):
-            h = 4 * part + i
-            rows.append(jnp.concatenate([H[2 * h], H[2 * h + 1]], axis=1))
+            j = 4 * part + i
+            rows.append(jnp.concatenate([H[2 * j], H[2 * j + 1]], axis=1))
         spectrum = dot3(jnp.concatenate(rows, axis=0), bh, bl, NT)
         for i in range(4):
-            h = 4 * part + i
-            ca, sa = AT[0, pl.ds(h, 1), :], AT[1, pl.ds(h, 1), :]
+            j = 4 * part + i
+            ca, sa = [jnp.concatenate([AP[p, j]] * 3, axis=0) for p in range(2)]
             yc = spectrum[24 * i : 24 * i + 24, :128]
             ys = spectrum[24 * i : 24 * i + 24, 128:]
             zr_sum += ca * yc + sa * ys
@@ -385,7 +413,9 @@
     HF[pl.ds(0, 24), :] = zr_sum * scale
     HF[pl.ds(24, 24), :] = zi_sum * scale
     HF[pl.ds(48, 16), :] = jnp.zeros((16, 128), F32)
-    mine = jnp.concatenate([HF[pl.ds(r, 8, stride=8), :] for r in range(2, 6)], axis=0)
+    mine = jnp.concatenate(
+        [HF[pl.ds(r, 8, stride=8), :] + HF[pl.ds(r + 4, 8, stride=8), :] for r in range(4)], axis=0
+    )
     S2[:, pl.ds(0, 32)] = mine.T
 
     send(S2, 1, G2, gs2, gr2)
@@ -439,15 +469,16 @@
         scratch_shapes=[
             V((2, 1, 1, 4, NDEG), BF16), pltpu.SMEM((NPOS,), jnp.int32), V((NLAT,), F32),
             pltpu.SMEM((8, 8), F32), pltpu.SMEM((8,), F32), pltpu.SMEM((3, 8), F32),
-            V((8, 8, NLON), F32), V((8, 8, NLON), F32), V((8, 8, NLON), F32), V((8, 8, NLON), F32),
-            V((8, NLON), F32), V((3, 8, NLON), F32), V((14, 8, 128), F32),
+            V((8, 8, NLON), F32), V((8, 8, NLON), F32), V((8, 8, NLON // 2), F32), V((8, 8, NLON), F32),
+            V((8, 8, NLON // 2), F32), V((8, NLON), F32), V((3, 8, NLON // 2), F32), V((14, 8, 128), F32),
+            V((2, 8, NLON // 2), F32), V((2, 8, 8, 128), F32),
             V((NDEG, NLAT), BF16), V((8, NDEG), F32),
             V((NLAT, 128), F32), V((NPOS, 128), F32),
             V((128, 128), F32),
             V((NL, 4, CHUNK), F32), V((NL, 4, CHUNK), F32), V((8, NLON), F32),
-            V((7, 8, NLON), F32),
+            V((6, 8, NLON), F32),
             V((2, 16, 128), F32), V((256, 256), BF16), V((256, 256), BF16),
-            V((32, 24, 128), F32), V((64, 128), F32),
+            V((16, 24, 128), F32), V((64, 128), F32),
             V((128, 128), F32), V((NPOS, 128), F32),
             V((NLAT, 128), F32), V((128, 128), jnp.int32),
             DMA((12,)), DMA((1,)), DMA((1,)), DMA((NL,)), DMA((NL,)),

time: 44.1 us -> 42.8 us (0.971)
  Pallas kernels: 43.3 us -> 42 us
    pallas_call x1, Pallas kernels: 42.5 us -> 41.1 us  [body(): pl.pallas_call(kernel, out_shape=(V((8, 1, 4, NLON), F32), V((2, 3, 1, 1,...]
where the time goes in v5:
time: 42.8 us; the launch traced here: 42.6 us
  Pallas kernels  42 us (98%)
  between operations  0.64 us (1%)
    pallas_call x1, Pallas kernels, body(): pl.pallas_call(kernel, out_shape=(V((8, 1, 4, NLON), F32), V((2, 3, 1, 1,...  41.1 us

profile of v5, /device:TPU:1, one launch (start us, length us, event | category | flops | bytes accessed | tf_op | source)
XLA Modules:
  0.0 42.6 jit_solution(4577581023989782232)
XLA Ops:
  0.6 41.1 %shard_map.95 = (f32[8,1,4,4096]{3,2,1,0:T(4,128)S(1)}, f32[2,3,1,1,1024]{4,3,2,1,0:T(1,128)S(1)}) custom-call(bf16[2,1,1,4,1024]{4,3,2,1,0:T(4,128)(2,1)} %bitcast.1, bf16[1,1024,384]{2,1,0:T(8,128)(2,1)} %leg.1, s32[96]{0:T(128)} %wn_in.1, f32[384]{0:T(512)} %quad_in.1, f32[8,1,4,4096]{3,2,1,0:T(4,128)} %trc.1, f32[8,8]{1,0:T(8,128)} %kin_in.1, f32[8]{0:T(128)} %pho_in.1, ...), custom_call_target="tpu_custom_call" | custom-call | tf_op jit(solution)/shard_map/pallas_call | solution.py:461
  41.8 0.8 %shard_map.96 = (f32[8,1,4,4096]{3,2,1,0:T(4,128)}, f32[2,3,1,1,1024]{4,3,2,1,0:T(1,128)}) custom-call(f32[8,1,4,4096]{3,2,1,0:T(4,128)S(1)} %get-tuple-element.4.tracers_ref, f32[2,3,1,1,1024]{4,3,2,1,0:T(1,128)S(1)} %get-tuple-element.5.heating_ref), custom_call_target="tpu_custom_call" | custom-call | tf_op jit(solution)/shard_map/pallas_call | solution.py:493

commit v6 on v5

--- a/solution.py
+++ b/solution.py
@@ -204,6 +204,21 @@
         return jnp.where(
             upper[:, : first.shape[1]], pltpu.roll(first, 6, 0), pltpu.roll(second, 2, 0)
         )
+
+    for k in range(1, NL):
+        l_copy(k, True).wait_recv()
+    total = jnp.zeros((4, CHUNK), F32)
+    for level in range(NL):
+        PC[level] = 0.2 * jnp.exp(total * (-2.0 / NL))
+        if level < NL - 1:
+            total += LR[level]
+    for k in FAR_L:
+        for side in range(2):
+            e_copy(side, k).start()
+        p_copy(k).start()
+    for side in range(2):
+        e_copy(side, 0).start()
+    PH[pl.ds(2, 4), pl.ds(pl.multiple_of(CHUNK * l, CHUNK), CHUNK)] = PC[l]
 
     for s in range(NPOS):
         WC[pl.ds(s, 1), :] = jnp.full((1, 128), wn[s], jnp.int32)
@@ -225,20 +240,6 @@
             hi, lo = split(jnp.where(used, table, 0.0))
             BH[pl.ds(128 * p, 128), pl.ds(128 * half, 128)] = hi
             BL[pl.ds(128 * p, 128), pl.ds(128 * half, 128)] = lo
-
-    for k in range(1, NL):
-        l_copy(k, True).wait_recv()
-    total = jnp.zeros((4, CHUNK), F32)
-    for level in range(NL):
-        PC[level] = 0.2 * jnp.exp(total * (-2.0 / NL))
-        if level < NL - 1:
-            total += LR[level]
-    for k in FAR_L:
-        p_copy(k).start()
-    for k in range(NL):
-        for side in range(2):
-            e_copy(side, k).start()
-    PH[pl.ds(2, 4), pl.ds(pl.multiple_of(CHUNK * l, CHUNK), CHUNK)] = PC[l]
 
     for copy in small[2:]:
         copy.wait()

time: 42.8 us -> 42.7 us (level)
  no operation moved by 1% of the time
where the time goes in v6:
time: 42.7 us; the launch traced here: 42.6 us
  Pallas kernels  41.9 us (98%)
  between operations  0.64 us (1%)
    pallas_call x1, Pallas kernels, body(): pl.pallas_call(kernel, out_shape=(V((8, 1, 4, NLON), F32), V((2, 3, 1, 1,...  41.1 us

profile of v6, /device:TPU:1, one launch (start us, length us, event | category | flops | bytes accessed | tf_op | source)
XLA Modules:
  0.0 42.6 jit_solution(17108917643339894868)
XLA Ops:
  0.6 41.1 %shard_map.95 = (f32[8,1,4,4096]{3,2,1,0:T(4,128)S(1)}, f32[2,3,1,1,1024]{4,3,2,1,0:T(1,128)S(1)}) custom-call(bf16[2,1,1,4,1024]{4,3,2,1,0:T(4,128)(2,1)} %bitcast.1, bf16[1,1024,384]{2,1,0:T(8,128)(2,1)} %leg.1, s32[96]{0:T(128)} %wn_in.1, f32[384]{0:T(512)} %quad_in.1, f32[8,1,4,4096]{3,2,1,0:T(4,128)} %trc.1, f32[8,8]{1,0:T(8,128)} %kin_in.1, f32[8]{0:T(128)} %pho_in.1, ...), custom_call_target="tpu_custom_call" | custom-call | tf_op jit(solution)/shard_map/pallas_call | solution.py:462
  41.8 0.8 %shard_map.96 = (f32[8,1,4,4096]{3,2,1,0:T(4,128)}, f32[2,3,1,1,1024]{4,3,2,1,0:T(1,128)}) custom-call(f32[8,1,4,4096]{3,2,1,0:T(4,128)S(1)} %get-tuple-element.4.tracers_ref, f32[2,3,1,1,1024]{4,3,2,1,0:T(1,128)S(1)} %get-tuple-element.5.heating_ref), custom_call_target="tpu_custom_call" | custom-call | tf_op jit(solution)/shard_map/pallas_call | solution.py:494
